TPU v7x, 16 devices: a whole 2x2x2 slice. The times are simulated.
16 devices in a mesh: data: 2 (over z), tp: 8 (over y, x, core).
Axes of the slice: x: 2, y: 2, z: 2, core: 2. Of those that a mesh axis runs over, the one named last changes fastest.
Arguments:
- x_in: bfloat16 [16384, 3072], P('data'), parts along dimension 0
- w_gate: bfloat16 [3072, 8192], P(None, 'tp')
- w_up: bfloat16 [3072, 8192], P(None, 'tp')
- w_down: bfloat16 [8192, 3072], P('tp')
- residual: bfloat16 [16384, 3072], P(('data', 'tp')), parts along dimension 0
- norm_gain: float32 [3072], replicated
Outputs:
- output 1: bfloat16 [16384, 3072], P(('data', 'tp')), parts along dimension 0
- output 2: bfloat16 [16384, 3072], P(('data', 'tp')), parts along dimension 0
There are 2 independent parts. A program takes and returns all parts, laid end to end along the dimension named above; an argument that names none is the same for every part.
All inputs are finite; a program needn't handle non-finite values.
Results may differ from a plain program's by a relative error of at most 0.00648036.
Values are sent between devices in bfloat16 or wider.
A program may use at most 1 GiB of HBM per device.

v0:
```python
import jax
import jax.numpy as jnp
from jax import lax
from jax.sharding import PartitionSpec as P

EPS = 1e-5


def add_and_norm(y_sum, residual, norm_gain):
    hidden_sum = residual.astype(jnp.float32) + y_sum
    mean_sq = jnp.mean(hidden_sum * hidden_sum, axis=-1, keepdims=True)
    normed = hidden_sum * lax.rsqrt(mean_sq + EPS) * norm_gain
    return hidden_sum.astype(jnp.bfloat16), normed.astype(jnp.bfloat16)


def solution(mesh):
    tp_size = mesh.shape["tp"]

    def local_block(x_in, w_gate, w_up, w_down, residual, norm_gain):
        gate_val = jnp.dot(x_in, w_gate, preferred_element_type=jnp.float32)
        up_val = jnp.dot(x_in, w_up, preferred_element_type=jnp.float32)
        hidden = (jax.nn.silu(gate_val) * up_val).astype(jnp.bfloat16)
        part_prod = jnp.dot(hidden, w_down, preferred_element_type=jnp.float32).astype(jnp.bfloat16)
        received = lax.all_to_all(part_prod, "tp", 0, 0, tiled=True)
        rows = residual.shape[0]
        y_sum = jnp.sum(received.reshape(tp_size, rows, received.shape[1]), axis=0, dtype=jnp.float32)
        return add_and_norm(y_sum, residual, norm_gain)

    row_spec = P(("data", "tp"), None)
    return jax.shard_map(local_block, mesh=mesh, in_specs=(P("data", None), P(None, "tp"), P(None, "tp"), P("tp", None), row_spec, P(None)), out_specs=(row_spec, row_spec), check_vma=False)
```

profile of v0, /device:TPU:1, one launch (start us, length us, event | category | flops | bytes accessed | tf_op | source)
XLA Modules:
  0.0 784.7 jit_solution(5690112922747863873)
XLA Ops:
  0.6 0.0 copy-start.1
  0.6 61.2 %fusion.2 = f32[8192,1024]{1,0:T(8,128)} fusion(bf16[8192,3072]{1,0:T(8,128)(2,1)} %param.6, bf16[3072,1024]{1,0:T(8,128)(2,1)} %param.7), kind=kOutput, calls=%fused_computation.9 | convolution fusion | flops 51539607552 | bytes 90177536 | tf_op jit(solution)/shard_map/dot_general | solution.py:20
  61.9 0.0 copy-done.1
  61.9 61.7 %multiply_convert_fusion.clone.4 = bf16[8192,1024]{1,0:T(8,128)(2,1)} fusion(f32[8192,1024]{1,0:T(8,128)} %fusion.2, bf16[8192,3072]{1,0:T(8,128)(2,1)} %param.6, bf16[3072,1024]{1,0:T(8,128)(2,1)S(1)} %copy-done.1), kind=kOutput, calls=%fused_computation.2.clone.clone.clone.1 | convolution fusion | flops 51589939200 | bytes 106954752 | tf_op jit(solution)/shard_map/dot_general | solution.py:21
  123.6 60.9 %convolution_convert_fusion = bf16[8192,3072]{1,0:T(8,128)(2,1)} fusion(bf16[1024,3072]{1,0:T(8,128)(2,1)} %param.9, bf16[8192,1024]{1,0:T(8,128)(2,1)} %multiply_convert_fusion.clone.4), kind=kOutput, calls=%fused_computation.1 | convolution fusion | flops 51564773376 | bytes 73400320 | tf_op jit(solution)/shard_map/dot_general | solution.py:23
  184.5 557.4 %all_to_all.9 = bf16[8,1024,3072]{2,1,0:T(8,128)(2,1)} all-to-all(bf16[8,1024,3072]{2,1,0:T(8,128)(2,1)} %bitcast.14), channel_id=1, replica_groups=mesh['data'=2,'tp'=8] {'tp'}, dimensions={0} | all-to-all | bytes 100663296 | tf_op jit(solution)/shard_map/all_to_all | solution.py:24
  741.9 21.6 %convert_reduce_fusion = f32[1024,3072]{1,0:T(8,128)} fusion(bf16[8,1024,3072]{2,1,0:T(8,128)(2,1)} %all_to_all.9), kind=kLoop, calls=%fused_computation | loop fusion | flops 47185920 | bytes 62914560 | tf_op jit(solution)/shard_map/reduce_sum | solution.py:26
  763.5 0.0 copy-start
  763.5 8.1 %multiply_reduce_fusion = f32[1024]{0:T(1024)S(1)} fusion(f32[1024,3072]{1,0:T(8,128)} %convert_reduce_fusion, bf16[1024,3072]{1,0:T(8,128)(2,1)} %param.10), kind=kLoop, calls=%fused_computation.4 | loop fusion | flops 12581888 | bytes 18878464 | tf_op jit(solution)/shard_map/reduce_sum | solution.py:11
  771.6 0.0 copy-done
  771.6 13.1 %multiply_convert_fusion.1 = (bf16[1024,3072]{1,0:T(8,128)(2,1)}, bf16[1024,3072]{1,0:T(8,128)(2,1)}) fusion(f32[3072]{0:T(1024)S(1)} %copy-done, f32[1024]{0:T(1024)S(1)} %add_rsqrt_fusion, f32[1024,3072]{1,0:T(8,128)} %convert_reduce_fusion, bf16[1024,3072]{1,0:T(8,128)(2,1)} %param.10), kind=kLoop, calls=%fused_computation.3 | loop fusion | flops 18874368 | bytes 31473664 | tf_op jit(solution)/shard_map/convert_element_type | solution.py:13
  (1 shorter events, 0.0 us)
Async XLA Ops:
  0.6 61.2 %copy-start.1 = (bf16[3072,1024]{1,0:T(8,128)(2,1)S(1)}, bf16[3072,1024]{1,0:T(8,128)(2,1)}, u32[]{:S(2)}) copy-start(bf16[3072,1024]{1,0:T(8,128)(2,1)} %param.8) | copy-start | bytes 18874372
  763.5 8.1 %copy-start = (f32[3072]{0:T(1024)S(1)}, f32[3072]{0:T(1024)}, u32[]{:S(2)}) copy-start(f32[3072]{0:T(1024)} %param.11) | copy-start | bytes 36868
where the time goes:
time: 787 us; the launch traced here: 785 us
  blocking collectives  557 us (71%)
  matrix products  184 us (23%)
  other arithmetic  42.8 us (5%)
    all_to_all x1, blocking collectives, local_block(): received = lax.all_to_all(part_prod, 'tp', 0, 0, tiled=True)  557 us
    dot_general x1, matrix products, local_block(): up_val = jnp.dot(x_in, w_up, preferred_element_type=jnp.float32)  61.7 us
    dot_general x1, matrix products, local_block(): gate_val = jnp.dot(x_in, w_gate, preferred_element_type=jnp.float32)  61.2 us
    dot_general x1, matrix products, local_block(): jnp.dot(hidden, w_down, preferred_element_type=jnp.float32)  60.9 us
    reduce_sum x1, other arithmetic, local_block(): jnp.sum(received.reshape(tp_size, rows, received.shape[1]), axis=0, dtype...  21.6 us

commit v1 on v0

v1 whole, which is shorter than its diff:
```python
import jax
import jax.numpy as jnp
from jax import lax
from jax.sharding import PartitionSpec as P

EPS = 1e-5


def solution(mesh):
    tp_size = mesh.shape["tp"]

    def local_block(x_in, w_gate, w_up, w_down, residual, norm_gain):
        w_all = lax.all_gather(w_down, "tp", axis=0)
        gate_val = jnp.dot(x_in, w_gate, preferred_element_type=jnp.float32)
        up_val = jnp.dot(x_in, w_up, preferred_element_type=jnp.float32)
        hidden = (jax.nn.silu(gate_val) * up_val).astype(jnp.bfloat16)
        rows = residual.shape[0]
        received = lax.all_to_all(hidden.reshape(tp_size, rows, -1), "tp", 0, 0, tiled=True)
        h = residual.astype(jnp.float32)
        total = jnp.zeros(h.shape, jnp.float32)
        for p in range(tp_size):
            part = jnp.dot(received[p], w_all[p], preferred_element_type=jnp.float32)
            total = total + lax.reduce_precision(part, 8, 7)
        h = h + total
        mean_sq = jnp.mean(h * h, axis=-1, keepdims=True)
        normed = h * lax.rsqrt(mean_sq + EPS) * norm_gain
        return h.astype(jnp.bfloat16), normed.astype(jnp.bfloat16)

    row_spec = P(("data", "tp"), None)
    return jax.shard_map(local_block, mesh=mesh, in_specs=(P("data", None), P(None, "tp"), P(None, "tp"), P("tp", None), row_spec, P(None)), out_specs=(row_spec, row_spec), check_vma=False)
```

time: 787 us -> 568 us (0.72)
  blocking collectives: 557 us -> 284 us
  matrix products: 184 us -> 247 us
  other arithmetic: 42.8 us -> 16.1 us
  between operations: 0.65 us -> 14.1 us
    all_to_all x1, blocking collectives: 557 us -> 284 us  [local_block(): lax.all_to_all(hidden.reshape(tp_size, rows, -1), 'tp', 0, 0, tiled=True)]
    dot_general x1 -> x8, matrix products: 60.9 us -> 125 us  [local_block(): part = jnp.dot(received[p], w_all[p], preferred_element_type=jnp.float32)]
    reduce_sum x2 -> x0, other arithmetic: 29.7 us -> none  [the longest x1 21.6 us: local_block(): jnp.sum(received.reshape(tp_size, rows, received.shape[1]), axis=0, dtype...]
  transfers between devices with their start and end apart: 0 -> 1, of which waited for: 0 -> 1; matrix products, arithmetic and copies ran while one was open for 0% -> 22% of each run, Pallas kernels for 0% -> 0%
where the time goes in v1:
time: 568 us; the launch traced here: 567 us
  blocking collectives  284 us (50%)
  matrix products  247 us (43%)
  other arithmetic  16.1 us (3%)
  between operations  14.1 us (2%)
    all_to_all x1, blocking collectives, local_block(): lax.all_to_all(hidden.reshape(tp_size, rows, -1), 'tp', 0, 0, tiled=True)  284 us
    dot_general x8, matrix products, local_block(): part = jnp.dot(received[p], w_all[p], preferred_element_type=jnp.float32)  125 us
    dot_general x1, matrix products, local_block(): up_val = jnp.dot(x_in, w_up, preferred_element_type=jnp.float32)  61.5 us
    dot_general x1, matrix products, local_block(): gate_val = jnp.dot(x_in, w_gate, preferred_element_type=jnp.float32)  61.2 us
    convert_element_type x1, other arithmetic, local_block(): return (h.astype(jnp.bfloat16), normed.astype(jnp.bfloat16))  16.1 us
  transfers between devices with their start and end apart: 1, of which 1 were waited for; matrix products, arithmetic and copies ran while one was open for 22% of the time, Pallas kernels for 0%

profile of v1, /device:TPU:1, one launch (start us, length us, event | category | flops | bytes accessed | tf_op | source)
XLA Modules:
  0.0 566.9 jit_solution(7448217766679172214)
XLA Ops:
  7.2 0.0 all-gather.3.cloned.1.call-start
  7.2 0.7 all-gather.3.cloned.1.call-update
  7.9 61.2 %fusion.15 = f32[8192,1024]{1,0:T(8,128)} fusion(bf16[8192,3072]{1,0:T(8,128)(2,1)} %param.6, bf16[3072,1024]{1,0:T(8,128)(2,1)} %param.7), kind=kOutput, calls=%fused_computation.28 | convolution fusion | flops 51539607552 | bytes 90177536 | tf_op jit(solution)/shard_map/dot_general | solution.py:14
  69.1 61.5 %multiply_convert_fusion = bf16[8192,1024]{1,0:T(8,128)(2,1)S(1)} fusion(f32[8192,1024]{1,0:T(8,128)} %fusion.15, bf16[8192,3072]{1,0:T(8,128)(2,1)} %param.6, bf16[3072,1024]{1,0:T(8,128)(2,1)} %param.8), kind=kOutput, calls=%fused_computation | convolution fusion | flops 51589939200 | bytes 106954752 | tf_op jit(solution)/shard_map/dot_general | solution.py:15
  130.6 284.5 %all_to_all.5 = bf16[8,1024,1024]{2,1,0:T(8,128)(2,1)} all-to-all(bf16[8,1024,1024]{2,1,0:T(8,128)(2,1)S(1)} %bitcast.31), channel_id=1, replica_groups=mesh['data'=2,'tp'=8] {'tp'}, dimensions={0} | all-to-all | bytes 33554432 | tf_op jit(solution)/shard_map/all_to_all | solution.py:18
  415.1 4.1 all-gather.3.cloned.1.call-done
  419.2 0.0 copy-start
  419.2 12.2 %fusion.1 = f32[1024,3072]{1,0:T(8,128)} fusion(bf16[8192,3072]{1,0:T(8,128)(2,1)} %all-gather.3.cloned.1.call-done, bf16[8,1024,1024]{2,1,0:T(8,128)(2,1)} %all_to_all.5), kind=kOutput, calls=%fused_computation.5 | convolution fusion | flops 6442450944 | bytes 20971520 | tf_op jit(solution)/shard_map/dot_general | solution.py:22
  431.3 0.0 copy-done
  431.3 12.3 %fusion.3 = f32[1024,3072]{1,0:T(8,128)} fusion(bf16[8192,3072]{1,0:T(8,128)(2,1)} %all-gather.3.cloned.1.call-done, bf16[8,1024,1024]{2,1,0:T(8,128)(2,1)S(1)} %copy-done), kind=kOutput, calls=%fused_computation.7 | convolution fusion | flops 6442450944 | bytes 20971520 | tf_op jit(solution)/shard_map/dot_general | solution.py:22
  443.6 12.2 %fusion.5 = f32[1024,3072]{1,0:T(8,128)} fusion(bf16[8192,3072]{1,0:T(8,128)(2,1)} %all-gather.3.cloned.1.call-done, bf16[8,1024,1024]{2,1,0:T(8,128)(2,1)S(1)} %copy-done), kind=kOutput, calls=%fused_computation.9 | convolution fusion | flops 6442450944 | bytes 20971520 | tf_op jit(solution)/shard_map/dot_general | solution.py:22
  455.9 12.3 %fusion.7 = f32[1024,3072]{1,0:T(8,128)} fusion(bf16[8192,3072]{1,0:T(8,128)(2,1)} %all-gather.3.cloned.1.call-done, bf16[8,1024,1024]{2,1,0:T(8,128)(2,1)S(1)} %copy-done), kind=kOutput, calls=%fused_computation.11 | convolution fusion | flops 6442450944 | bytes 20971520 | tf_op jit(solution)/shard_map/dot_general | solution.py:22
  468.2 12.2 %fusion.9 = f32[1024,3072]{1,0:T(8,128)} fusion(bf16[8192,3072]{1,0:T(8,128)(2,1)} %all-gather.3.cloned.1.call-done, bf16[8,1024,1024]{2,1,0:T(8,128)(2,1)S(1)} %copy-done), kind=kOutput, calls=%fused_computation.13 | convolution fusion | flops 6442450944 | bytes 20971520 | tf_op jit(solution)/shard_map/dot_general | solution.py:22
  480.4 12.2 %fusion.11 = f32[1024,3072]{1,0:T(8,128)} fusion(bf16[8192,3072]{1,0:T(8,128)(2,1)} %all-gather.3.cloned.1.call-done, bf16[8,1024,1024]{2,1,0:T(8,128)(2,1)S(1)} %copy-done), kind=kOutput, calls=%fused_computation.15 | convolution fusion | flops 6442450944 | bytes 20971520 | tf_op jit(solution)/shard_map/dot_general | solution.py:22
  492.6 12.3 %fusion.13 = f32[1024,3072]{1,0:T(8,128)} fusion(bf16[8192,3072]{1,0:T(8,128)(2,1)} %all-gather.3.cloned.1.call-done, bf16[8,1024,1024]{2,1,0:T(8,128)(2,1)S(1)} %copy-done), kind=kOutput, calls=%fused_computation.17 | convolution fusion | flops 6442450944 | bytes 20971520 | tf_op jit(solution)/shard_map/dot_general | solution.py:22
  504.9 0.0 copy-start.1
  504.9 39.0 %multiply_reduce_fusion = (f32[1024]{0:T(1024)S(1)}, f32[1024,3072]{1,0:T(8,128)}) fusion(bf16[8192,3072]{1,0:T(8,128)(2,1)} %all-gather.3.cloned.1.call-done, bf16[8,1024,1024]{2,1,0:T(8,128)(2,1)} %all_to_all.5, f32[1024,3072]{1,0:T(8,128)} %fusion.1, f32[1024,3072]{1,0:T(8,128)} %fusion.3, f32[1024,3072]{1,0:T(8,128)} %fusion.5, f32[1024,3072]{1,0:T(8,128)} %fusion.7, ...), kind=kOutput, calls=%fused_computation.2 | convolution fusion | flops 6502218752 | bytes 115347456 | tf_op jit(solution)/shard_map/dot_general | solution.py:22
  543.9 0.0 copy-done.1
  543.9 16.1 %multiply_convert_fusion.1 = (bf16[1024,3072]{1,0:T(8,128)(2,1)}, bf16[1024,3072]{1,0:T(8,128)(2,1)}) fusion(f32[1024,3072]{1,0:T(8,128)} %get-tuple-element.5, f32[3072]{0:T(1024)S(1)} %copy-done.1, f32[1024]{0:T(1024)S(1)} %add_rsqrt_fusion), kind=kLoop, calls=%fused_computation.1 | loop fusion | flops 12582912 | bytes 25182208 | tf_op jit(solution)/shard_map/convert_element_type | solution.py:27
  (1 shorter events, 0.0 us)
Async XLA Ops:
  7.2 412.0 %all-gather.3.cloned.1.call-start = ((), (), s32[]{:S(2)}) async-start(), calls=%async_computation.1 | async-start | bytes 56623104 | tf_op jit(solution)/shard_map/all_gather | solution.py:13
  419.2 12.2 %copy-start = (bf16[8,1024,1024]{2,1,0:T(8,128)(2,1)S(1)}, bf16[8,1024,1024]{2,1,0:T(8,128)(2,1)}, u32[]{:S(2)}) copy-start(bf16[8,1024,1024]{2,1,0:T(8,128)(2,1)} %all_to_all.5) | copy-start | bytes 50331652
  504.9 39.0 %copy-start.1 = (f32[3072]{0:T(1024)S(1)}, f32[3072]{0:T(1024)}, u32[]{:S(2)}) copy-start(f32[3072]{0:T(1024)} %param.11) | copy-start | bytes 36868
Sparse Core Ops, SparseCore 0:
  9.8 409.2 all-gather.2

commit v2 on v0

v2 whole, which is shorter than its diff:
```python
import functools

import jax
import jax.numpy as jnp
from jax import lax
from jax.experimental import pallas as pl
from jax.experimental.pallas import tpu as pltpu
from jax.sharding import PartitionSpec as P

EPS = 1e-5
MESH = pl.DeviceIdType.MESH
F32 = jnp.float32
BF16 = jnp.bfloat16


def block_kernel(x_ref, wg_ref, wu_ref, wd_ref, res_ref, gain_ref, h_ref, n_ref, wall_ref, gout, gin, w_send, w_recv, g_send, g_recv):
    p = lax.axis_index("tp")
    z = lax.axis_index("data")
    core, px, py = p % 2, (p // 2) % 2, p // 4
    rows = wd_ref.shape[0]
    half, quarter = rows // 2, rows // 4
    cols = wg_ref.shape[1]
    width = wd_ref.shape[1]
    blocks = 16

    def peer(r):
        return p + (r % 2) * (1 - 2 * core) + ((r // 2) % 2) * (2 - 4 * px) + (r // 4) * (4 - 8 * py)

    def tp(r):
        return {"tp": peer(r)}

    twin = {"data": 1 - z}

    barrier = pltpu.get_barrier_semaphore()
    for r in range(1, 8):
        pl.semaphore_signal(barrier, inc=1, device_id=tp(r), device_id_type=MESH)
    pl.semaphore_signal(barrier, inc=1, device_id=twin, device_id_type=MESH)
    pl.semaphore_wait(barrier, 8)

    mine, other = z * half, (1 - z) * half
    q0, q1 = pl.ds(mine, quarter), pl.ds(mine + quarter, quarter)
    hm, ho = pl.ds(mine, half), pl.ds(other, half)
    whole = pl.ds(0, rows)
    events = [
        (0, 2, q0, tp(2)),
        (0, 2, q1, tp(2)),
        (0, 4, q1, tp(4)),
        (0, 4, q0, tp(4)),
        (0, 1, whole, tp(1)),
        (2, 6, q0, tp(4)),
        (2, 2, q0, twin),
        (4, 6, q1, tp(2)),
        (4, 4, q1, twin),
        (2, 2, q1, twin),
        (2, 3, hm, tp(1)),
        (4, 4, q0, twin),
        (4, 5, hm, tp(1)),
        (6, 6, q0, twin),
        (6, 6, q1, twin),
        (6, 7, hm, tp(1)),
        (2, 3, ho, tp(1)),
        (4, 5, ho, tp(1)),
        (6, 7, ho, tp(1)),
    ]

    def w_copy(e):
        src, dst, where, target = events[e]
        src_ref = wd_ref.at[where] if src == 0 else wall_ref.at[src, where]
        return pltpu.make_async_remote_copy(src_ref=src_ref, dst_ref=wall_ref.at[dst, where], send_sem=w_send.at[e], recv_sem=w_recv.at[e], device_id=target, device_id_type=MESH)

    def w_start(*ids):
        for e in ids:
            w_copy(e).start()

    def w_wait(*ids):
        for e in ids:
            w_copy(e).wait_recv()

    def place(j):
        m = j % 6
        t = m % 3
        r = jnp.where(j < 12, 6 - 4 * t + 6 * (t // 2) + m // 3, 1 - (j - 12) // 2)
        return r, jnp.where(j < 12, j // 6, j % 2)

    def g_copy(j, r, h):
        return pltpu.make_async_remote_copy(src_ref=gout.at[j], dst_ref=gin.at[r - 1, pl.ds(h * half, half)], send_sem=g_send.at[j], recv_sem=g_recv.at[r * 2 + h], device_id=tp(r), device_id_type=MESH)

    w_start(0, 2, 1, 3, 4)

    def produce(xbuf, wg, wu, x_sem, wg_sem, wu_sem):
        def x_copy(j):
            r, h = place(j)
            start = pl.multiple_of(peer(r) * rows + h * half, half)
            return pltpu.make_async_copy(x_ref.at[pl.ds(start, half)], xbuf.at[j % 2], x_sem.at[j % 2])

        wg_copy = pltpu.make_async_copy(wg_ref, wg, wg_sem)
        wu_copy = pltpu.make_async_copy(wu_ref, wu, wu_sem)
        x_copy(0).start()
        wg_copy.start()
        wu_copy.start()
        wg_copy.wait()
        wu_copy.wait()

        def step(j, carry):
            x_copy(j).wait()

            @pl.when(j + 1 < blocks)
            def _():
                x_copy(j + 1).start()

            @pl.loop(0, cols // 256)
            def _(n):
                tile = pl.ds(pl.multiple_of(n * 256, 256), 256)
                xb = xbuf[j % 2]
                gate = jnp.dot(xb, wg[:, tile], preferred_element_type=F32)
                up = jnp.dot(xb, wu[:, tile], preferred_element_type=F32)
                gout[j, :, tile] = (jax.nn.silu(gate) * up).astype(BF16)

            r, h = place(j)

            @pl.when(j < 14)
            def _():
                g_copy(j, r, h).start()

            @pl.when(j == 5)
            def _():
                w_wait(0, 2)
                w_start(5, 7, 6, 8)

            @pl.when(j == 10)
            def _():
                w_wait(1, 3)
                w_start(9, 11, 10, 12)

            return carry

        lax.fori_loop(0, blocks, step, 0)

    pl.run_scoped(
        produce,
        pltpu.VMEM((2, half, wg_ref.shape[0]), BF16),
        pltpu.VMEM(wg_ref.shape, BF16),
        pltpu.VMEM(wu_ref.shape, BF16),
        pltpu.SemaphoreType.DMA((2,)),
        pltpu.SemaphoreType.DMA,
        pltpu.SemaphoreType.DMA,
    )

    def consume(acc, wbuf, wb_sem, res_sem, out_sem):
        tile_n = 512

        def load(r, slot):
            src = wd_ref if r == 0 else wall_ref.at[r]
            return pltpu.make_async_copy(src, wbuf.at[slot], wb_sem.at[slot])

        def add(r, h, slot, first=False):
            if r:
                g_copy(0, r, h).wait_recv()
            top = h * half

            @pl.loop(0, width // tile_n)
            def _(n):
                tile = pl.ds(pl.multiple_of(n * tile_n, tile_n), tile_n)
                act = gout[14 + h] if r == 0 else gin[r - 1, pl.ds(top, half)]
                part = jnp.dot(act, wbuf[slot, :, tile], preferred_element_type=F32).astype(BF16).astype(F32)
                if first:
                    acc[pl.ds(top, half), tile] = part
                else:
                    acc[pl.ds(top, half), tile] += part

        def finish(h):
            top = h * half
            chunk, sub = 128, 32
            res = pltpu.make_async_copy(res_ref.at[pl.ds(top, half)], wbuf.at[1, pl.ds(0, half)], res_sem)
            res.start()
            res.wait()
            copies = []
            for k in range(half // chunk):
                @pl.loop(0, chunk // sub)
                def _(i):
                    at = pl.multiple_of(k * chunk + i * sub, sub)
                    h32 = wbuf[1, pl.ds(at, sub)].astype(F32) + acc[pl.ds(top + at, sub)]
                    mean_sq = jnp.sum(h32 * h32, axis=-1, keepdims=True) * (1.0 / width)
                    wbuf[0, pl.ds(at, sub)] = h32.astype(BF16)
                    wbuf[0, pl.ds(half + at, sub)] = (h32 * lax.rsqrt(mean_sq + EPS) * gain_ref[...]).astype(BF16)

                place_out = pl.ds(top + k * chunk, chunk)
                copies.append(pltpu.make_async_copy(wbuf.at[0, pl.ds(k * chunk, chunk)], h_ref.at[place_out], out_sem.at[2 * k]))
                copies.append(pltpu.make_async_copy(wbuf.at[0, pl.ds(half + k * chunk, chunk)], n_ref.at[place_out], out_sem.at[2 * k + 1]))
                copies[-2].start()
                copies[-1].start()
            for copy in copies:
                copy.wait()

        def run(steps, first=False):
            load(steps[0][0], 0).start()
            for i, (r, halves) in enumerate(steps):
                load(r, i % 2).wait()
                if i + 1 < len(steps):
                    load(steps[i + 1][0], (i + 1) % 2).start()
                for h in halves:
                    add(r, h, i % 2, first and i == 0)

        w_wait(4)
        run([(0, (0, 1)), (1, (0, 1))], first=True)
        w_wait(5, 7)
        w_start(13, 14, 15)
        w_wait(6, 9)
        w_start(16)
        w_wait(8, 11)
        w_start(17)
        w_wait(10, 16, 12, 17)
        run([(2, (0,)), (4, (0,)), (3, (0,)), (5, (0,))])
        w_wait(13, 14)
        w_start(18)
        w_wait(15, 18)
        run([(6, (0,)), (7, (0,))])
        finish(0)
        run([(6, (1,)), (2, (1,)), (4, (1,)), (7, (1,)), (3, (1,)), (5, (1,))])
        finish(1)

    pl.run_scoped(
        consume,
        pltpu.VMEM((rows, width), F32),
        pltpu.VMEM((2, rows, width), BF16),
        pltpu.SemaphoreType.DMA((2,)),
        pltpu.SemaphoreType.DMA,
        pltpu.SemaphoreType.DMA((8,)),
    )

    for e in range(len(events)):
        w_copy(e).wait_send()

    def drain(j, carry):
        r, h = place(j)
        g_copy(j, r, h).wait_send()
        return carry

    lax.fori_loop(0, 14, drain, 0)


def solution(mesh):
    def local_block(x_in, w_gate, w_up, w_down, residual, norm_gain):
        rows, width = residual.shape
        cols = w_gate.shape[1]
        any_spec = pl.BlockSpec(memory_space=pl.ANY)
        h_out, normed, _ = pl.pallas_call(
            block_kernel,
            out_shape=(
                jax.ShapeDtypeStruct((rows, width), BF16),
                jax.ShapeDtypeStruct((rows, width), BF16),
                jax.ShapeDtypeStruct((8, rows, width), BF16),
            ),
            in_specs=[any_spec] * 5 + [pl.BlockSpec(memory_space=pltpu.VMEM)],
            out_specs=(any_spec, any_spec, any_spec),
            scratch_shapes=[
                pltpu.VMEM((16, rows // 2, cols), BF16),
                pltpu.VMEM((7, rows, cols), BF16),
                pltpu.SemaphoreType.DMA((19,)),
                pltpu.SemaphoreType.DMA((19,)),
                pltpu.SemaphoreType.DMA((16,)),
                pltpu.SemaphoreType.DMA((16,)),
            ],
            compiler_params=pltpu.CompilerParams(collective_id=0, has_side_effects=True, vmem_limit_bytes=66_000_000),
        )(x_in, w_gate, w_up, w_down, residual, norm_gain.reshape(1, width))
        return h_out, normed

    row_spec = P(("data", "tp"), None)
    return jax.shard_map(local_block, mesh=mesh, in_specs=(P("data", None), P(None, "tp"), P(None, "tp"), P("tp", None), row_spec, P(None)), out_specs=(row_spec, row_spec), check_vma=False)
```

time: 787 us -> 334 us (0.42)
  blocking collectives: 557 us -> 0 us
  Pallas kernels: 0 us -> 324 us
  matrix products: 184 us -> 0 us
  other arithmetic: 42.8 us -> 0 us
  local copies, waits for them, and re-layouts: 0.01 us -> 8.82 us
    all_to_all x1 -> x0, blocking collectives: 557 us -> none  [local_block(): received = lax.all_to_all(part_prod, 'tp', 0, 0, tiled=True)]
    pallas_call x0 -> x1, Pallas kernels: none -> 324 us  [local_block(): pl.pallas_call(block_kernel, out_shape=(jax.ShapeDtypeStruct((rows, width...]
    dot_general x3 -> x0, matrix products: 184 us -> none  [the longest x1 61.7 us: local_block(): up_val = jnp.dot(x_in, w_up, preferred_element_type=jnp.float32)]
    reduce_sum x2 -> x0, other arithmetic: 29.7 us -> none  [the longest x1 21.6 us: local_block(): jnp.sum(received.reshape(tp_size, rows, received.shape[1]), axis=0, dtype...]
    convert_element_type x1 -> x0, other arithmetic: 13.1 us -> none  [add_and_norm(): return (hidden_sum.astype(jnp.bfloat16), normed.astype(jnp.bfloat16))]
    unnamed x4, local copies, waits for them, and re-layouts: 0.01 us -> 8.82 us
where the time goes in v2:
time: 334 us
  Pallas kernels  324 us (97%)
  local copies, waits for them, and re-layouts  8.82 us (3%)
    pallas_call x1, Pallas kernels, local_block(): pl.pallas_call(block_kernel, out_shape=(jax.ShapeDtypeStruct((rows, width...  324 us
    unnamed x4, local copies, waits for them, and re-layouts  8.82 us

profile of v2, /device:TPU:1, one launch (start us, length us, event | category | flops | bytes accessed | tf_op | source)
XLA Modules:
  0.0 333.9 jit_solution(9607970983203356246)
XLA Ops:
  0.6 324.4 %shard_map.77 = (bf16[1024,3072]{1,0:T(8,128)(2,1)}, bf16[1024,3072]{1,0:T(8,128)(2,1)}, bf16[8,1024,3072]{2,1,0:T(8,128)(2,1)}) custom-call(bf16[8192,3072]{1,0:T(8,128)(2,1)} %x_ref.1, bf16[3072,1024]{1,0:T(8,128)(2,1)} %wg_ref.1, bf16[3072,1024]{1,0:T(8,128)(2,1)} %wu_ref.1, bf16[1024,3072]{1,0:T(8,128)(2,1)} %wd_ref.1, bf16[1024,3072]{1,0:T(8,128)(2,1)} %res_ref.1, ...), custom_call_target="tpu_custom_call" | custom-call | tf_op jit(solution)/shard_map/pallas_call | solution.py:247
  325.1 0.0 copy-start
  325.1 6.1 %copy.10 = bf16[1024,3072]{1,0:T(8,128)(2,1)} copy(bf16[1024,3072]{1,0:T(8,128)(2,1)} %get-tuple-element.8) | data formatting | bytes 12582912
  331.2 0.0 copy-done
  331.2 2.7 copy.11
Async XLA Ops:
  325.1 6.1 %copy-start = (bf16[1024,3072]{1,0:T(8,128)(2,1)S(1)}, bf16[1024,3072]{1,0:T(8,128)(2,1)}, u32[]{:S(2)}) copy-start(bf16[1024,3072]{1,0:T(8,128)(2,1)} %get-tuple-element.9) | copy-start | bytes 18874372

commit v3 on v2

--- a/solution.py
+++ b/solution.py
@@ -22,6 +22,7 @@
     cols = wg_ref.shape[1]
     width = wd_ref.shape[1]
     blocks = 16
+    gate_step = 4
 
     def peer(r):
         return p + (r % 2) * (1 - 2 * core) + ((r // 2) % 2) * (2 - 4 * px) + (r // 4) * (4 - 8 * py)
@@ -30,12 +31,6 @@
         return {"tp": peer(r)}
 
     twin = {"data": 1 - z}
-
-    barrier = pltpu.get_barrier_semaphore()
-    for r in range(1, 8):
-        pl.semaphore_signal(barrier, inc=1, device_id=tp(r), device_id_type=MESH)
-    pl.semaphore_signal(barrier, inc=1, device_id=twin, device_id_type=MESH)
-    pl.semaphore_wait(barrier, 8)
 
     mine, other = z * half, (1 - z) * half
     q0, q1 = pl.ds(mine, quarter), pl.ds(mine + quarter, quarter)
@@ -77,15 +72,20 @@
             w_copy(e).wait_recv()
 
     def place(j):
-        m = j % 6
-        t = m % 3
-        r = jnp.where(j < 12, 6 - 4 * t + 6 * (t // 2) + m // 3, 1 - (j - 12) // 2)
-        return r, jnp.where(j < 12, j // 6, j % 2)
-
-    def g_copy(j, r, h):
-        return pltpu.make_async_remote_copy(src_ref=gout.at[j], dst_ref=gin.at[r - 1, pl.ds(h * half, half)], send_sem=g_send.at[j], recv_sem=g_recv.at[r * 2 + h], device_id=tp(r), device_id_type=MESH)
-
-    w_start(0, 2, 1, 3, 4)
+        near_r, near_h = 2 + 2 * (j % 2) + (j % 4) // 2, j // 4
+        far_r, far_h = 6 + j % 2, (j - 8) // 2
+        r = jnp.where(j < 8, near_r, jnp.where(j < 12, far_r, 1 - (j - 12) // 2))
+        return r, jnp.where(j < 8, near_h, jnp.where(j < 12, far_h, j % 2))
+
+    def g_copy(j, r, h, s):
+        src = gout.at[j, pl.ds(s * quarter, quarter)]
+        dst = gin.at[r - 1, pl.ds(h * half + s * quarter, quarter)]
+        return pltpu.make_async_remote_copy(src_ref=src, dst_ref=dst, send_sem=g_send.at[2 * j + s], recv_sem=g_recv.at[4 * r + 2 * h + s], device_id=tp(r), device_id_type=MESH)
+
+    def g_start(j):
+        r, h = place(j)
+        for s in range(2):
+            g_copy(j, r, h, s).start()
 
     def produce(xbuf, wg, wu, x_sem, wg_sem, wu_sem):
         def x_copy(j):
@@ -98,8 +98,20 @@
         x_copy(0).start()
         wg_copy.start()
         wu_copy.start()
+
+        barrier = pltpu.get_barrier_semaphore()
+        for r in range(1, 8):
+            pl.semaphore_signal(barrier, inc=1, device_id=tp(r), device_id_type=MESH)
+        pl.semaphore_signal(barrier, inc=1, device_id=twin, device_id_type=MESH)
+        pl.semaphore_wait(barrier, 8)
+
+        w_start(0, 2, 1, 3, 4)
         wg_copy.wait()
         wu_copy.wait()
+
+        def send(j, carry):
+            g_start(j)
+            return carry
 
         def step(j, carry):
             x_copy(j).wait()
@@ -116,18 +128,17 @@
                 up = jnp.dot(xb, wu[:, tile], preferred_element_type=F32)
                 gout[j, :, tile] = (jax.nn.silu(gate) * up).astype(BF16)
 
-            r, h = place(j)
-
-            @pl.when(j < 14)
-            def _():
-                g_copy(j, r, h).start()
-
-            @pl.when(j == 5)
+            @pl.when(j == gate_step)
             def _():
                 w_wait(0, 2)
                 w_start(5, 7, 6, 8)
-
-            @pl.when(j == 10)
+                lax.fori_loop(0, gate_step, send, 0)
+
+            @pl.when((j >= gate_step) & (j < 14))
+            def _():
+                g_start(j)
+
+            @pl.when(j == 9)
             def _():
                 w_wait(1, 3)
                 w_start(9, 11, 10, 12)
@@ -146,51 +157,61 @@
         pltpu.SemaphoreType.DMA,
     )
 
-    def consume(acc, wbuf, wb_sem, res_sem, out_sem):
+    def consume(acc, wbuf, rbuf, wb_sem, res_sem, out_sem):
         tile_n = 512
 
         def load(r, slot):
             src = wd_ref if r == 0 else wall_ref.at[r]
             return pltpu.make_async_copy(src, wbuf.at[slot], wb_sem.at[slot])
 
-        def add(r, h, slot, first=False):
+        def add(r, h, slot, first=False, part=None):
+            subs = (0, 1) if part is None else (part,)
             if r:
-                g_copy(0, r, h).wait_recv()
-            top = h * half
+                for s in subs:
+                    g_copy(0, r, h, s).wait_recv()
+            count = quarter * len(subs)
+            inner = pl.ds(subs[0] * quarter, count)
+            outer = pl.ds(h * half + subs[0] * quarter, count)
 
             @pl.loop(0, width // tile_n)
             def _(n):
                 tile = pl.ds(pl.multiple_of(n * tile_n, tile_n), tile_n)
-                act = gout[14 + h] if r == 0 else gin[r - 1, pl.ds(top, half)]
-                part = jnp.dot(act, wbuf[slot, :, tile], preferred_element_type=F32).astype(BF16).astype(F32)
+                act = gout[14 + h, inner] if r == 0 else gin[r - 1, outer]
+                prod = jnp.dot(act, wbuf[slot, :, tile], preferred_element_type=F32).astype(BF16).astype(F32)
                 if first:
-                    acc[pl.ds(top, half), tile] = part
+                    acc[outer, tile] = prod
                 else:
-                    acc[pl.ds(top, half), tile] += part
-
-        def finish(h):
-            top = h * half
-            chunk, sub = 128, 32
-            res = pltpu.make_async_copy(res_ref.at[pl.ds(top, half)], wbuf.at[1, pl.ds(0, half)], res_sem)
-            res.start()
-            res.wait()
-            copies = []
-            for k in range(half // chunk):
+                    acc[outer, tile] += prod
+
+        def res_copy(h):
+            return pltpu.make_async_copy(res_ref.at[pl.ds(h * half, half)], rbuf, res_sem)
+
+        def out_copies(h, k):
+            there = pl.ds(h * half + k * chunk, chunk)
+            return (
+                pltpu.make_async_copy(wbuf.at[0, pl.ds(k * chunk, chunk)], h_ref.at[there], out_sem.at[2 * k]),
+                pltpu.make_async_copy(wbuf.at[0, pl.ds(half + k * chunk, chunk)], n_ref.at[there], out_sem.at[2 * k + 1]),
+            )
+
+        chunk, sub = 128, 32
+
+        def finish(h, ks):
+            for k in ks:
                 @pl.loop(0, chunk // sub)
                 def _(i):
                     at = pl.multiple_of(k * chunk + i * sub, sub)
-                    h32 = wbuf[1, pl.ds(at, sub)].astype(F32) + acc[pl.ds(top + at, sub)]
+                    h32 = rbuf[pl.ds(at, sub)].astype(F32) + acc[pl.ds(h * half + at, sub)]
                     mean_sq = jnp.sum(h32 * h32, axis=-1, keepdims=True) * (1.0 / width)
                     wbuf[0, pl.ds(at, sub)] = h32.astype(BF16)
                     wbuf[0, pl.ds(half + at, sub)] = (h32 * lax.rsqrt(mean_sq + EPS) * gain_ref[...]).astype(BF16)
 
-                place_out = pl.ds(top + k * chunk, chunk)
-                copies.append(pltpu.make_async_copy(wbuf.at[0, pl.ds(k * chunk, chunk)], h_ref.at[place_out], out_sem.at[2 * k]))
-                copies.append(pltpu.make_async_copy(wbuf.at[0, pl.ds(half + k * chunk, chunk)], n_ref.at[place_out], out_sem.at[2 * k + 1]))
-                copies[-2].start()
-                copies[-1].start()
-            for copy in copies:
-                copy.wait()
+                for copy in out_copies(h, k):
+                    copy.start()
+
+        def finish_wait(h):
+            for k in range(half // chunk):
+                for copy in out_copies(h, k):
+                    copy.wait()
 
         def run(steps, first=False):
             load(steps[0][0], 0).start()
@@ -201,28 +222,44 @@
                 for h in halves:
                     add(r, h, i % 2, first and i == 0)
 
+        res_copy(0).start()
+        w_wait(5, 7)
+        w_start(13, 14, 15)
         w_wait(4)
         run([(0, (0, 1)), (1, (0, 1))], first=True)
-        w_wait(5, 7)
-        w_start(13, 14, 15)
         w_wait(6, 9)
         w_start(16)
         w_wait(8, 11)
         w_start(17)
+        run([(2, (0,)), (4, (0,))])
         w_wait(10, 16, 12, 17)
-        run([(2, (0,)), (4, (0,)), (3, (0,)), (5, (0,))])
+        run([(3, (0,)), (5, (0,)), (2, (1,)), (4, (1,)), (3, (1,)), (5, (1,))])
         w_wait(13, 14)
         w_start(18)
+        load(6, 0).start()
+        load(6, 0).wait()
+        add(6, 0, 0)
         w_wait(15, 18)
-        run([(6, (0,)), (7, (0,))])
-        finish(0)
-        run([(6, (1,)), (2, (1,)), (4, (1,)), (7, (1,)), (3, (1,)), (5, (1,))])
-        finish(1)
+        load(7, 1).start()
+        load(7, 1).wait()
+        add(7, 0, 1)
+        add(6, 1, 0)
+        res_copy(0).wait()
+        finish(0, range(4))
+        res_copy(1).start()
+        add(7, 1, 1, part=0)
+        finish_wait(0)
+        res_copy(1).wait()
+        finish(1, (0, 1))
+        add(7, 1, 1, part=1)
+        finish(1, (2, 3))
+        finish_wait(1)
 
     pl.run_scoped(
         consume,
         pltpu.VMEM((rows, width), F32),
         pltpu.VMEM((2, rows, width), BF16),
+        pltpu.VMEM((half, width), BF16),
         pltpu.SemaphoreType.DMA((2,)),
         pltpu.SemaphoreType.DMA,
         pltpu.SemaphoreType.DMA((8,)),
@@ -233,7 +270,8 @@
 
     def drain(j, carry):
         r, h = place(j)
-        g_copy(j, r, h).wait_send()
+        for s in range(2):
+            g_copy(j, r, h, s).wait_send()
         return carry
 
     lax.fori_loop(0, 14, drain, 0)
@@ -258,8 +296,8 @@
                 pltpu.VMEM((7, rows, cols), BF16),
                 pltpu.SemaphoreType.DMA((19,)),
                 pltpu.SemaphoreType.DMA((19,)),
-                pltpu.SemaphoreType.DMA((16,)),
-                pltpu.SemaphoreType.DMA((16,)),
+                pltpu.SemaphoreType.DMA((32,)),
+                pltpu.SemaphoreType.DMA((32,)),
             ],
             compiler_params=pltpu.CompilerParams(collective_id=0, has_side_effects=True, vmem_limit_bytes=66_000_000),
         )(x_in, w_gate, w_up, w_down, residual, norm_gain.reshape(1, width))

time: 334 us -> 303 us (0.907)
  Pallas kernels: 324 us -> 293 us
    pallas_call x1, Pallas kernels: 324 us -> 293 us  [local_block(): pl.pallas_call(block_kernel, out_shape=(jax.ShapeDtypeStruct((rows, width...]
where the time goes in v3:
time: 303 us
  Pallas kernels  293 us (97%)
  local copies, waits for them, and re-layouts  8.82 us (3%)
    pallas_call x1, Pallas kernels, local_block(): pl.pallas_call(block_kernel, out_shape=(jax.ShapeDtypeStruct((rows, width...  293 us
    unnamed x4, local copies, waits for them, and re-layouts  8.82 us

profile of v3, /device:TPU:1, one launch (start us, length us, event | category | flops | bytes accessed | tf_op | source)
XLA Modules:
  0.0 302.7 jit_solution(2273612591023515437)
XLA Ops:
  0.6 293.2 %shard_map.77 = (bf16[1024,3072]{1,0:T(8,128)(2,1)}, bf16[1024,3072]{1,0:T(8,128)(2,1)}, bf16[8,1024,3072]{2,1,0:T(8,128)(2,1)}) custom-call(bf16[8192,3072]{1,0:T(8,128)(2,1)} %x_ref.1, bf16[3072,1024]{1,0:T(8,128)(2,1)} %wg_ref.1, bf16[3072,1024]{1,0:T(8,128)(2,1)} %wu_ref.1, bf16[1024,3072]{1,0:T(8,128)(2,1)} %wd_ref.1, bf16[1024,3072]{1,0:T(8,128)(2,1)} %res_ref.1, ...), custom_call_target="tpu_custom_call" | custom-call | tf_op jit(solution)/shard_map/pallas_call | solution.py:285
  293.9 0.0 copy-start
  293.9 6.1 %copy.10 = bf16[1024,3072]{1,0:T(8,128)(2,1)} copy(bf16[1024,3072]{1,0:T(8,128)(2,1)} %get-tuple-element.8) | data formatting | bytes 12582912
  300.0 0.0 copy-done
  300.0 2.7 copy.11
Async XLA Ops:
  293.9 6.1 %copy-start = (bf16[1024,3072]{1,0:T(8,128)(2,1)S(1)}, bf16[1024,3072]{1,0:T(8,128)(2,1)}, u32[]{:S(2)}) copy-start(bf16[1024,3072]{1,0:T(8,128)(2,1)} %get-tuple-element.9) | copy-start | bytes 18874372

commit v4 on v3

--- a/solution.py
+++ b/solution.py
@@ -18,7 +18,7 @@
     z = lax.axis_index("data")
     core, px, py = p % 2, (p // 2) % 2, p // 4
     rows = wd_ref.shape[0]
-    half, quarter = rows // 2, rows // 4
+    half, quarter, piece = rows // 2, rows // 4, rows // 8
     cols = wg_ref.shape[1]
     width = wd_ref.shape[1]
     blocks = 16
@@ -78,13 +78,13 @@
         return r, jnp.where(j < 8, near_h, jnp.where(j < 12, far_h, j % 2))
 
     def g_copy(j, r, h, s):
-        src = gout.at[j, pl.ds(s * quarter, quarter)]
-        dst = gin.at[r - 1, pl.ds(h * half + s * quarter, quarter)]
-        return pltpu.make_async_remote_copy(src_ref=src, dst_ref=dst, send_sem=g_send.at[2 * j + s], recv_sem=g_recv.at[4 * r + 2 * h + s], device_id=tp(r), device_id_type=MESH)
+        src = gout.at[j, pl.ds(s * piece, piece)]
+        dst = gin.at[r - 1, pl.ds(h * half + s * piece, piece)]
+        return pltpu.make_async_remote_copy(src_ref=src, dst_ref=dst, send_sem=g_send.at[4 * j + s], recv_sem=g_recv.at[8 * r + 4 * h + s], device_id=tp(r), device_id_type=MESH)
 
     def g_start(j):
         r, h = place(j)
-        for s in range(2):
+        for s in range(4):
             g_copy(j, r, h, s).start()
 
     def produce(xbuf, wg, wu, x_sem, wg_sem, wu_sem):
@@ -157,61 +157,50 @@
         pltpu.SemaphoreType.DMA,
     )
 
-    def consume(acc, wbuf, rbuf, wb_sem, res_sem, out_sem):
+    def consume(acc, wbuf, rbuf, wb_sem, res_sem):
         tile_n = 512
 
         def load(r, slot):
             src = wd_ref if r == 0 else wall_ref.at[r]
-            return pltpu.make_async_copy(src, wbuf.at[slot], wb_sem.at[slot])
-
-        def add(r, h, slot, first=False, part=None):
-            subs = (0, 1) if part is None else (part,)
+            return pltpu.make_async_copy(src, (h_ref, wbuf)[slot], wb_sem.at[slot])
+
+        def add(r, h, slot, first=False, subs=(0, 1, 2, 3)):
             if r:
                 for s in subs:
                     g_copy(0, r, h, s).wait_recv()
-            count = quarter * len(subs)
-            inner = pl.ds(subs[0] * quarter, count)
-            outer = pl.ds(h * half + subs[0] * quarter, count)
+            count = piece * len(subs)
+            inner = pl.ds(subs[0] * piece, count)
+            outer = pl.ds(h * half + subs[0] * piece, count)
 
             @pl.loop(0, width // tile_n)
             def _(n):
                 tile = pl.ds(pl.multiple_of(n * tile_n, tile_n), tile_n)
                 act = gout[14 + h, inner] if r == 0 else gin[r - 1, outer]
-                prod = jnp.dot(act, wbuf[slot, :, tile], preferred_element_type=F32).astype(BF16).astype(F32)
+                prod = jnp.dot(act, (h_ref, wbuf)[slot][:, tile], preferred_element_type=F32).astype(BF16).astype(F32)
                 if first:
                     acc[outer, tile] = prod
                 else:
                     acc[outer, tile] += prod
 
-        def res_copy(h):
-            return pltpu.make_async_copy(res_ref.at[pl.ds(h * half, half)], rbuf, res_sem)
-
-        def out_copies(h, k):
-            there = pl.ds(h * half + k * chunk, chunk)
-            return (
-                pltpu.make_async_copy(wbuf.at[0, pl.ds(k * chunk, chunk)], h_ref.at[there], out_sem.at[2 * k]),
-                pltpu.make_async_copy(wbuf.at[0, pl.ds(half + k * chunk, chunk)], n_ref.at[there], out_sem.at[2 * k + 1]),
-            )
+        def res_copy(h, k):
+            return pltpu.make_async_copy(res_ref.at[pl.ds(h * half + k * chunk, chunk)], rbuf.at[k % 2], res_sem.at[k % 2])
 
         chunk, sub = 128, 32
 
         def finish(h, ks):
             for k in ks:
+                res_copy(h, k).wait()
                 @pl.loop(0, chunk // sub)
                 def _(i):
-                    at = pl.multiple_of(k * chunk + i * sub, sub)
-                    h32 = rbuf[pl.ds(at, sub)].astype(F32) + acc[pl.ds(h * half + at, sub)]
+                    at = pl.multiple_of(i * sub, sub)
+                    there = pl.ds(h * half + k * chunk + at, sub)
+                    h32 = rbuf[k % 2, pl.ds(at, sub)].astype(F32) + acc[there]
                     mean_sq = jnp.sum(h32 * h32, axis=-1, keepdims=True) * (1.0 / width)
-                    wbuf[0, pl.ds(at, sub)] = h32.astype(BF16)
-                    wbuf[0, pl.ds(half + at, sub)] = (h32 * lax.rsqrt(mean_sq + EPS) * gain_ref[...]).astype(BF16)
-
-                for copy in out_copies(h, k):
-                    copy.start()
-
-        def finish_wait(h):
-            for k in range(half // chunk):
-                for copy in out_copies(h, k):
-                    copy.wait()
+                    h_ref[there] = h32.astype(BF16)
+                    n_ref[there] = (h32 * lax.rsqrt(mean_sq + EPS) * gain_ref[...]).astype(BF16)
+
+                if 4 * h + k + 2 < 8:
+                    res_copy(h + (k + 2) // 4, (k + 2) % 4).start()
 
         def run(steps, first=False):
             load(steps[0][0], 0).start()
@@ -222,7 +211,8 @@
                 for h in halves:
                     add(r, h, i % 2, first and i == 0)
 
-        res_copy(0).start()
+        res_copy(0, 0).start()
+        res_copy(0, 1).start()
         w_wait(5, 7)
         w_start(13, 14, 15)
         w_wait(4)
@@ -244,25 +234,21 @@
         load(7, 1).wait()
         add(7, 0, 1)
         add(6, 1, 0)
-        res_copy(0).wait()
         finish(0, range(4))
-        res_copy(1).start()
-        add(7, 1, 1, part=0)
-        finish_wait(0)
-        res_copy(1).wait()
+        add(7, 1, 1, subs=(0, 1))
         finish(1, (0, 1))
-        add(7, 1, 1, part=1)
-        finish(1, (2, 3))
-        finish_wait(1)
+        add(7, 1, 1, subs=(2,))
+        finish(1, (2,))
+        add(7, 1, 1, subs=(3,))
+        finish(1, (3,))
 
     pl.run_scoped(
         consume,
         pltpu.VMEM((rows, width), F32),
-        pltpu.VMEM((2, rows, width), BF16),
-        pltpu.VMEM((half, width), BF16),
+        pltpu.VMEM((rows, width), BF16),
+        pltpu.VMEM((2, 128, width), BF16),
         pltpu.SemaphoreType.DMA((2,)),
-        pltpu.SemaphoreType.DMA,
-        pltpu.SemaphoreType.DMA((8,)),
+        pltpu.SemaphoreType.DMA((2,)),
     )
 
     for e in range(len(events)):
@@ -270,7 +256,7 @@
 
     def drain(j, carry):
         r, h = place(j)
-        for s in range(2):
+        for s in range(4):
             g_copy(j, r, h, s).wait_send()
         return carry
 
@@ -282,24 +268,25 @@
         rows, width = residual.shape
         cols = w_gate.shape[1]
         any_spec = pl.BlockSpec(memory_space=pl.ANY)
+        vm = pl.BlockSpec(memory_space=pltpu.VMEM)
         h_out, normed, _ = pl.pallas_call(
             block_kernel,
             out_shape=(
-                jax.ShapeDtypeStruct((rows, width), BF16),
-                jax.ShapeDtypeStruct((rows, width), BF16),
+                pltpu.VMEM((rows, width), BF16),
+                pltpu.VMEM((rows, width), BF16),
                 jax.ShapeDtypeStruct((8, rows, width), BF16),
             ),
             in_specs=[any_spec] * 5 + [pl.BlockSpec(memory_space=pltpu.VMEM)],
-            out_specs=(any_spec, any_spec, any_spec),
+            out_specs=(vm, vm, any_spec),
             scratch_shapes=[
                 pltpu.VMEM((16, rows // 2, cols), BF16),
                 pltpu.VMEM((7, rows, cols), BF16),
                 pltpu.SemaphoreType.DMA((19,)),
                 pltpu.SemaphoreType.DMA((19,)),
-                pltpu.SemaphoreType.DMA((32,)),
-                pltpu.SemaphoreType.DMA((32,)),
+                pltpu.SemaphoreType.DMA((64,)),
+                pltpu.SemaphoreType.DMA((64,)),
             ],
-            compiler_params=pltpu.CompilerParams(collective_id=0, has_side_effects=True, vmem_limit_bytes=66_000_000),
+            compiler_params=pltpu.CompilerParams(collective_id=0, has_side_effects=True, vmem_limit_bytes=53_700_000),
         )(x_in, w_gate, w_up, w_down, residual, norm_gain.reshape(1, width))
         return h_out, normed
 

time: 303 us -> 298 us (0.983)
  local copies, waits for them, and re-layouts: 8.82 us -> 5.41 us
    unnamed x4 -> x2, local copies, waits for them, and re-layouts: 8.82 us -> 5.41 us
where the time goes in v4:
time: 298 us; the launch traced here: 297 us
  Pallas kernels  291 us (98%)
  local copies, waits for them, and re-layouts  5.41 us (2%)
    pallas_call x1, Pallas kernels, local_block(): pl.pallas_call(block_kernel, out_shape=(pltpu.VMEM((rows, width), BF16),...  291 us

profile of v4, /device:TPU:1, one launch (start us, length us, event | category | flops | bytes accessed | tf_op | source)
XLA Modules:
  0.0 297.3 jit_solution(1322427878579107156)
XLA Ops:
  0.6 291.3 %shard_map.77 = (bf16[1024,3072]{1,0:T(8,128)(2,1)S(1)}, bf16[1024,3072]{1,0:T(8,128)(2,1)S(1)}, bf16[8,1024,3072]{2,1,0:T(8,128)(2,1)}) custom-call(bf16[8192,3072]{1,0:T(8,128)(2,1)} %x_ref.1, bf16[3072,1024]{1,0:T(8,128)(2,1)} %wg_ref.1, bf16[3072,1024]{1,0:T(8,128)(2,1)} %wu_ref.1, bf16[1024,3072]{1,0:T(8,128)(2,1)} %wd_ref.1, ...), custom_call_target="tpu_custom_call" | custom-call | tf_op jit(solution)/shard_map/pallas_call | solution.py:272
  291.9 2.7 copy.10
  294.6 2.7 copy.11

commit v5 on v4

--- a/solution.py
+++ b/solution.py
@@ -13,7 +13,7 @@
 BF16 = jnp.bfloat16
 
 
-def block_kernel(x_ref, wg_ref, wu_ref, wd_ref, res_ref, gain_ref, h_ref, n_ref, wall_ref, gout, gin, w_send, w_recv, g_send, g_recv):
+def block_kernel(x_ref, wg_ref, wu_ref, wd_ref, res_ref, gain_ref, h_ref, n_ref, wbuf, part_ref, act_ref, rbuf, wall_ref, gout, gin, w_send, w_recv, g_send, g_recv):
     p = lax.axis_index("tp")
     z = lax.axis_index("data")
     core, px, py = p % 2, (p // 2) % 2, p // 4
@@ -87,11 +87,16 @@
         for s in range(4):
             g_copy(j, r, h, s).start()
 
-    def produce(xbuf, wg, wu, x_sem, wg_sem, wu_sem):
+    def g_wait_send(j):
+        r, h = place(j)
+        for s in range(4):
+            g_copy(j, r, h, s).wait_send()
+
+    def produce(wg, wu, x_sem, wg_sem, wu_sem):
         def x_copy(j):
             r, h = place(j)
             start = pl.multiple_of(peer(r) * rows + h * half, half)
-            return pltpu.make_async_copy(x_ref.at[pl.ds(start, half)], xbuf.at[j % 2], x_sem.at[j % 2])
+            return pltpu.make_async_copy(x_ref.at[pl.ds(start, half)], n_ref.at[pl.ds((j % 2) * half, half)], x_sem.at[j % 2])
 
         wg_copy = pltpu.make_async_copy(wg_ref, wg, wg_sem)
         wu_copy = pltpu.make_async_copy(wu_ref, wu, wu_sem)
@@ -115,18 +120,23 @@
 
         def step(j, carry):
             x_copy(j).wait()
+            slot = jnp.where(j < 14, j, j - 2)
 
             @pl.when(j + 1 < blocks)
             def _():
                 x_copy(j + 1).start()
+
+            @pl.when(j >= 14)
+            def _():
+                g_wait_send(j - 2)
 
             @pl.loop(0, cols // 256)
             def _(n):
                 tile = pl.ds(pl.multiple_of(n * 256, 256), 256)
-                xb = xbuf[j % 2]
+                xb = n_ref[pl.ds(pl.multiple_of((j % 2) * half, half), half)]
                 gate = jnp.dot(xb, wg[:, tile], preferred_element_type=F32)
                 up = jnp.dot(xb, wu[:, tile], preferred_element_type=F32)
-                gout[j, :, tile] = (jax.nn.silu(gate) * up).astype(BF16)
+                gout[slot, :, tile] = (jax.nn.silu(gate) * up).astype(BF16)
 
             @pl.when(j == gate_step)
             def _():
@@ -149,7 +159,6 @@
 
     pl.run_scoped(
         produce,
-        pltpu.VMEM((2, half, wg_ref.shape[0]), BF16),
         pltpu.VMEM(wg_ref.shape, BF16),
         pltpu.VMEM(wu_ref.shape, BF16),
         pltpu.SemaphoreType.DMA((2,)),
@@ -157,7 +166,7 @@
         pltpu.SemaphoreType.DMA,
     )
 
-    def consume(acc, wbuf, rbuf, wb_sem, res_sem):
+    def consume(acc, wb_sem, res_sem):
         tile_n = 512
 
         def load(r, slot):
@@ -175,7 +184,7 @@
             @pl.loop(0, width // tile_n)
             def _(n):
                 tile = pl.ds(pl.multiple_of(n * tile_n, tile_n), tile_n)
-                act = gout[14 + h, inner] if r == 0 else gin[r - 1, outer]
+                act = gout[12 + h, inner] if r == 0 else gin[r - 1, outer]
                 prod = jnp.dot(act, (h_ref, wbuf)[slot][:, tile], preferred_element_type=F32).astype(BF16).astype(F32)
                 if first:
                     acc[outer, tile] = prod
@@ -185,7 +194,7 @@
         def res_copy(h, k):
             return pltpu.make_async_copy(res_ref.at[pl.ds(h * half + k * chunk, chunk)], rbuf.at[k % 2], res_sem.at[k % 2])
 
-        chunk, sub = 128, 32
+        chunk, sub = 64, 32
 
         def finish(h, ks):
             for k in ks:
@@ -199,8 +208,8 @@
                     h_ref[there] = h32.astype(BF16)
                     n_ref[there] = (h32 * lax.rsqrt(mean_sq + EPS) * gain_ref[...]).astype(BF16)
 
-                if 4 * h + k + 2 < 8:
-                    res_copy(h + (k + 2) // 4, (k + 2) % 4).start()
+                if 8 * h + k + 2 < 16:
+                    res_copy(h + (k + 2) // 8, (k + 2) % 8).start()
 
         def run(steps, first=False):
             load(steps[0][0], 0).start()
@@ -234,19 +243,21 @@
         load(7, 1).wait()
         add(7, 0, 1)
         add(6, 1, 0)
-        finish(0, range(4))
+        finish(0, range(8))
         add(7, 1, 1, subs=(0, 1))
-        finish(1, (0, 1))
+        finish(1, range(4))
         add(7, 1, 1, subs=(2,))
-        finish(1, (2,))
-        add(7, 1, 1, subs=(3,))
-        finish(1, (3,))
+        finish(1, (4, 5))
+        tail = pl.ds(rows - piece, piece)
+        part_ref[...] = acc[tail]
+        res_copy(1, 6).wait()
+        res_copy(1, 7).wait()
+        g_copy(0, 7, 1, 3).wait_recv()
+        act_ref[...] = gin[6, tail]
 
     pl.run_scoped(
         consume,
         pltpu.VMEM((rows, width), F32),
-        pltpu.VMEM((rows, width), BF16),
-        pltpu.VMEM((2, 128, width), BF16),
         pltpu.SemaphoreType.DMA((2,)),
         pltpu.SemaphoreType.DMA((2,)),
     )
@@ -255,12 +266,45 @@
         w_copy(e).wait_send()
 
     def drain(j, carry):
-        r, h = place(j)
-        for s in range(4):
-            g_copy(j, r, h, s).wait_send()
+        g_wait_send(j)
         return carry
 
-    lax.fori_loop(0, 14, drain, 0)
+    lax.fori_loop(0, 12, drain, 0)
+
+
+def tail_kernel(h_ref, n_ref, w_ref, part_ref, act_ref, res_ref, gain_ref, h_out, n_out, total, tail_h, tail_n, sem):
+    rows, width = h_ref.shape
+    piece = part_ref.shape[0]
+    done, tail = pl.ds(0, rows - piece), pl.ds(rows - piece, piece)
+    copies = [
+        pltpu.make_async_copy(h_ref.at[done], h_out.at[done], sem.at[0]),
+        pltpu.make_async_copy(n_ref.at[done], n_out.at[done], sem.at[1]),
+        pltpu.make_async_copy(tail_h, h_out.at[tail], sem.at[2]),
+        pltpu.make_async_copy(tail_n, n_out.at[tail], sem.at[3]),
+    ]
+    copies[0].start()
+    copies[1].start()
+    tile_n, sub = 512, 32
+
+    @pl.loop(0, width // tile_n)
+    def _(n):
+        tile = pl.ds(pl.multiple_of(n * tile_n, tile_n), tile_n)
+        prod = jnp.dot(act_ref[...], w_ref[:, tile], preferred_element_type=F32)
+        total[:, tile] = part_ref[:, tile] + prod.astype(BF16).astype(F32)
+
+    @pl.loop(0, piece // sub)
+    def _(i):
+        at = pl.ds(pl.multiple_of(i * sub, sub), sub)
+        within = pl.ds(pl.multiple_of((i % 2) * sub, sub), sub)
+        h32 = res_ref[i // 2, within].astype(F32) + total[at]
+        mean_sq = jnp.sum(h32 * h32, axis=-1, keepdims=True) * (1.0 / width)
+        tail_h[at] = h32.astype(BF16)
+        tail_n[at] = (h32 * lax.rsqrt(mean_sq + EPS) * gain_ref[...]).astype(BF16)
+
+    copies[2].start()
+    copies[3].start()
+    for copy in copies:
+        copy.wait()
 
 
 def solution(mesh):
@@ -269,26 +313,44 @@
         cols = w_gate.shape[1]
         any_spec = pl.BlockSpec(memory_space=pl.ANY)
         vm = pl.BlockSpec(memory_space=pltpu.VMEM)
-        h_out, normed, _ = pl.pallas_call(
+        piece = rows // 8
+        gain = norm_gain.reshape(1, width)
+        *held, _ = pl.pallas_call(
             block_kernel,
             out_shape=(
                 pltpu.VMEM((rows, width), BF16),
                 pltpu.VMEM((rows, width), BF16),
+                pltpu.VMEM((rows, width), BF16),
+                pltpu.VMEM((piece, width), F32),
+                pltpu.VMEM((piece, cols), BF16),
+                pltpu.VMEM((2, piece // 2, width), BF16),
                 jax.ShapeDtypeStruct((8, rows, width), BF16),
             ),
-            in_specs=[any_spec] * 5 + [pl.BlockSpec(memory_space=pltpu.VMEM)],
-            out_specs=(vm, vm, any_spec),
+            in_specs=[any_spec] * 5 + [vm],
+            out_specs=(vm,) * 6 + (any_spec,),
             scratch_shapes=[
-                pltpu.VMEM((16, rows // 2, cols), BF16),
+                pltpu.VMEM((14, rows // 2, cols), BF16),
                 pltpu.VMEM((7, rows, cols), BF16),
                 pltpu.SemaphoreType.DMA((19,)),
                 pltpu.SemaphoreType.DMA((19,)),
                 pltpu.SemaphoreType.DMA((64,)),
                 pltpu.SemaphoreType.DMA((64,)),
             ],
-            compiler_params=pltpu.CompilerParams(collective_id=0, has_side_effects=True, vmem_limit_bytes=53_700_000),
-        )(x_in, w_gate, w_up, w_down, residual, norm_gain.reshape(1, width))
-        return h_out, normed
+            compiler_params=pltpu.CompilerParams(collective_id=0, has_side_effects=True, vmem_limit_bytes=45_100_000),
+        )(x_in, w_gate, w_up, w_down, residual, gain)
+        return pl.pallas_call(
+            tail_kernel,
+            out_shape=(jax.ShapeDtypeStruct((rows, width), BF16), jax.ShapeDtypeStruct((rows, width), BF16)),
+            in_specs=[vm] * 7,
+            out_specs=(any_spec, any_spec),
+            scratch_shapes=[
+                pltpu.VMEM((piece, width), F32),
+                pltpu.VMEM((piece, width), BF16),
+                pltpu.VMEM((piece, width), BF16),
+                pltpu.SemaphoreType.DMA((4,)),
+            ],
+            compiler_params=pltpu.CompilerParams(vmem_limit_bytes=8_000_000),
+        )(*held, gain)
 
     row_spec = P(("data", "tp"), None)
     return jax.shard_map(local_block, mesh=mesh, in_specs=(P("data", None), P(None, "tp"), P(None, "tp"), P("tp", None), row_spec, P(None)), out_specs=(row_spec, row_spec), check_vma=False)

time: 298 us -> 294 us (0.987)
  local copies, waits for them, and re-layouts: 5.41 us -> 0.01 us
    unnamed x2, local copies, waits for them, and re-layouts: 5.41 us -> 0.01 us
    pallas_call x0 -> x1, Pallas kernels: none -> 4.62 us  [local_block(): pl.pallas_call(tail_kernel, out_shape=(jax.ShapeDtypeStruct((rows, width)...]
where the time goes in v5:
time: 294 us
  Pallas kernels  293 us (100%)
    pallas_call x1, Pallas kernels, local_block(): pl.pallas_call(block_kernel, out_shape=(pltpu.VMEM((rows, width), BF16),...  289 us

profile of v5, /device:TPU:1, one launch (start us, length us, event | category | flops | bytes accessed | tf_op | source)
XLA Modules:
  0.0 294.0 jit_solution(10356714690432355225)
XLA Ops:
  0.6 0.0 copy-start
  0.6 288.8 %shard_map.77 = (bf16[1024,3072]{1,0:T(8,128)(2,1)S(1)}, bf16[1024,3072]{1,0:T(8,128)(2,1)S(1)}, bf16[1024,3072]{1,0:T(8,128)(2,1)S(1)}, f32[128,3072]{1,0:T(8,1...) custom-call(bf16[8192,3072]{1,0:T(8,128)(2,1)} %x_ref.1, ...), custom_call_target="tpu_custom_call" | custom-call | tf_op jit(solution)/shard_map/pallas_call | solution.py:318
  289.4 0.0 copy-done
  289.4 4.6 %shard_map.78 = (bf16[1024,3072]{1,0:T(8,128)(2,1)}, bf16[1024,3072]{1,0:T(8,128)(2,1)}) custom-call(bf16[1024,3072]{1,0:T(8,128)(2,1)S(1)} %get-tuple-element.8.h_ref, bf16[1024,3072]{1,0:T(8,128)(2,1)S(1)} %get-tuple-element.9.n_ref, bf16[1024,3072]{1,0:T(8,128)(2,1)S(1)} %get-tuple-element.10.w_ref, f32[128,3072]{1,0:T(8,128)S(1)} %get-tuple-element.11.part_ref, ...), custom_call_target="tpu_custom_call" | custom-call | tf_op jit(solution)/shard_map/pallas_call | solution.py:341
Async XLA Ops:
  0.6 288.8 %copy-start = (f32[3072]{0:T(1024)S(1)}, f32[3072]{0:T(1024)}, u32[]{:S(2)}) copy-start(f32[3072]{0:T(1024)} %param.11) | copy-start | bytes 36868

commit v6 on v5

--- a/solution.py
+++ b/solution.py
@@ -13,7 +13,7 @@
 BF16 = jnp.bfloat16
 
 
-def block_kernel(x_ref, wg_ref, wu_ref, wd_ref, res_ref, gain_ref, h_ref, n_ref, wbuf, part_ref, act_ref, rbuf, wall_ref, gout, gin, w_send, w_recv, g_send, g_recv):
+def block_kernel(x_ref, wg_ref, wu_ref, wd_ref, res_ref, gain_ref, h_ref, n_ref, wbuf, part_ref, act_ref, wall_ref, gout, gin, w_send, w_recv, g_send, g_recv, q_send, q_recv, s_send, s_recv):
     p = lax.axis_index("tp")
     z = lax.axis_index("data")
     core, px, py = p % 2, (p // 2) % 2, p // 4
@@ -22,7 +22,10 @@
     cols = wg_ref.shape[1]
     width = wd_ref.shape[1]
     blocks = 16
-    gate_step = 4
+    own_cols = cols * 3 // 4
+    share = cols - own_cols
+    depth = wg_ref.shape[0]
+    deep = depth // 6
 
     def peer(r):
         return p + (r % 2) * (1 - 2 * core) + ((r // 2) % 2) * (2 - 4 * px) + (r // 4) * (4 - 8 * py)
@@ -33,7 +36,8 @@
     twin = {"data": 1 - z}
 
     mine, other = z * half, (1 - z) * half
-    q0, q1 = pl.ds(mine, quarter), pl.ds(mine + quarter, quarter)
+    first = 13 * rows // 64
+    q0, q1 = pl.ds(mine, first), pl.ds(mine + first, half - first)
     hm, ho = pl.ds(mine, half), pl.ds(other, half)
     whole = pl.ds(0, rows)
     events = [
@@ -72,25 +76,56 @@
             w_copy(e).wait_recv()
 
     def place(j):
-        near_r, near_h = 2 + 2 * (j % 2) + (j % 4) // 2, j // 4
-        far_r, far_h = 6 + j % 2, (j - 8) // 2
-        r = jnp.where(j < 8, near_r, jnp.where(j < 12, far_r, 1 - (j - 12) // 2))
-        return r, jnp.where(j < 8, near_h, jnp.where(j < 12, far_h, j % 2))
-
-    def g_copy(j, r, h, s):
-        src = gout.at[j, pl.ds(s * piece, piece)]
-        dst = gin.at[r - 1, pl.ds(h * half + s * piece, piece)]
-        return pltpu.make_async_remote_copy(src_ref=src, dst_ref=dst, send_sem=g_send.at[4 * j + s], recv_sem=g_recv.at[8 * r + 4 * h + s], device_id=tp(r), device_id_type=MESH)
-
-    def g_start(j):
+        g = j // 4
+        return jnp.where(j < 12, 2 + 4 * g - 6 * (g // 2) + (j // 2) % 2, 1 - (j - 12) // 2), j % 2
+
+    def g_copy(j, r, h, count):
+        src = gout.at[j, :, pl.ds(0, count)]
+        dst = gin.at[r - 1, pl.ds(h * half, half), pl.ds(0, count)]
+        return pltpu.make_async_remote_copy(src_ref=src, dst_ref=dst, send_sem=g_send.at[j], recv_sem=g_recv.at[2 * r + h], device_id=tp(r), device_id_type=MESH)
+
+    def g_start(j, count):
         r, h = place(j)
-        for s in range(4):
-            g_copy(j, r, h, s).start()
-
-    def g_wait_send(j):
+        g_copy(j, r, h, count).start()
+
+    def g_wait_send(j, count):
         r, h = place(j)
-        for s in range(4):
-            g_copy(j, r, h, s).wait_send()
+        g_copy(j, r, h, count).wait_send()
+
+    def last_copy(s):
+        where = pl.ds(s * piece, piece)
+        src = gout.at[7, where, pl.ds(0, own_cols)]
+        dst = gin.at[6, pl.ds(half + s * piece, piece), pl.ds(0, own_cols)]
+        return pltpu.make_async_remote_copy(src_ref=src, dst_ref=dst, send_sem=g_send.at[14 + s], recv_sem=g_recv.at[16 + s], device_id=tp(7), device_id_type=MESH)
+
+    def stage(j):
+        return jnp.where(j < 12, j - 4, j - 10)
+
+    def s_copy(j, r, h):
+        shared = pl.ds(own_cols, share)
+        return pltpu.make_async_remote_copy(src_ref=gout.at[stage(j), :, shared], dst_ref=gin.at[r + 1, pl.ds(h * half, half), shared], send_sem=s_send.at[j - 8], recv_sem=s_recv.at[2 * r + h], device_id=tp(r), device_id_type=MESH)
+
+    def s_start(j):
+        r, h = place(j)
+        s_copy(j, r, h).start()
+
+    def q_where(k):
+        at = (k % 2) * (depth // 2) + (3 * z + k // 2) * share
+        return wbuf.at[pl.ds(0, deep), pl.ds(pl.multiple_of(at, share), share)]
+
+    def q_copy(k, src, sem, target):
+        return pltpu.make_async_remote_copy(src_ref=src, dst_ref=q_where(k), send_sem=q_send.at[sem], recv_sem=q_recv.at[sem], device_id=target, device_id_type=MESH)
+
+    def q_first(k):
+        src = (wg_ref, wu_ref)[k % 2]
+        at = pl.multiple_of((3 * z + k // 2) * deep, deep)
+        return q_copy(k, src.at[pl.ds(at, deep), pl.ds(own_cols, share)], k, tp(2))
+
+    def q_arrived(k):
+        return q_copy(k, q_where(k), k, tp(2))
+
+    def q_swap(k):
+        return q_copy(k, q_where(k), 6 + k, twin)
 
     def produce(wg, wu, x_sem, wg_sem, wu_sem):
         def x_copy(j):
@@ -110,17 +145,26 @@
         pl.semaphore_signal(barrier, inc=1, device_id=twin, device_id_type=MESH)
         pl.semaphore_wait(barrier, 8)
 
+        for k in range(6):
+            q_first(k).start()
         w_start(0, 2, 1, 3, 4)
         wg_copy.wait()
         wu_copy.wait()
 
-        def send(j, carry):
-            g_start(j)
+        def send_near(j, carry):
+            g_start(j, own_cols)
+            return carry
+
+        def send_wide(j, carry):
+            g_start(j, cols)
+            s_start(j)
             return carry
 
         def step(j, carry):
             x_copy(j).wait()
             slot = jnp.where(j < 14, j, j - 2)
+            r, h = place(j)
+            xrows = pl.ds(pl.multiple_of((j % 2) * half, half), half)
 
             @pl.when(j + 1 < blocks)
             def _():
@@ -128,30 +172,92 @@
 
             @pl.when(j >= 14)
             def _():
-                g_wait_send(j - 2)
-
-            @pl.loop(0, cols // 256)
+                g_wait_send(j - 2, cols)
+
+            @pl.loop(0, 3)
             def _(n):
                 tile = pl.ds(pl.multiple_of(n * 256, 256), 256)
-                xb = n_ref[pl.ds(pl.multiple_of((j % 2) * half, half), half)]
+                xb = n_ref[xrows]
                 gate = jnp.dot(xb, wg[:, tile], preferred_element_type=F32)
                 up = jnp.dot(xb, wu[:, tile], preferred_element_type=F32)
                 gout[slot, :, tile] = (jax.nn.silu(gate) * up).astype(BF16)
 
-            @pl.when(j == gate_step)
-            def _():
-                w_wait(0, 2)
-                w_start(5, 7, 6, 8)
-                lax.fori_loop(0, gate_step, send, 0)
-
-            @pl.when((j >= gate_step) & (j < 14))
-            def _():
-                g_start(j)
+            @pl.when(j >= 8)
+            def _():
+                tile = pl.ds(own_cols, share)
+                xb = n_ref[xrows]
+                gate = jnp.dot(xb, wg[:, tile], preferred_element_type=F32)
+                up = jnp.dot(xb, wu[:, tile], preferred_element_type=F32)
+                gout[slot, :, tile] = (jax.nn.silu(gate) * up).astype(BF16)
+
+            @pl.when(j < 6)
+            def _():
+                q_arrived(j).wait_recv()
+                q_swap(j).start()
+
+            @pl.when(j == 6)
+            def _():
+                w_wait(2)
+                w_start(7, 8)
+
+            @pl.when(j == 7)
+            def _():
+                lax.fori_loop(0, 7, send_near, 0)
+                for s in range(4):
+                    last_copy(s).start()
+
+            @pl.when(j == 8)
+            def _():
+                for k in range(6):
+                    q_swap(k).wait()
 
             @pl.when(j == 9)
             def _():
-                w_wait(1, 3)
-                w_start(9, 11, 10, 12)
+                w_wait(0)
+                w_start(5, 6)
+
+            @pl.when(j >= 8)
+            def _():
+                @pl.loop(0, 4)
+                def _(t):
+                    top = t * piece
+                    xt = pl.ds(pl.multiple_of((j % 2) * half + top, piece), piece)
+
+                    def product(base):
+                        total = None
+                        for k in range(6):
+                            part = jnp.dot(n_ref[xt, k * deep:(k + 1) * deep], wbuf[0:deep, base + k * share:base + (k + 1) * share], preferred_element_type=F32)
+                            total = part if total is None else total + part
+                        return total
+
+                    val = (jax.nn.silu(product(0)) * product(depth // 2)).astype(BF16)
+
+                    @pl.when(j < 14)
+                    def _():
+                        gout[stage(j), pl.ds(pl.multiple_of(top, piece), piece), own_cols:] = val
+
+                    @pl.when(j >= 14)
+                    def _():
+                        gin[1, pl.ds(pl.multiple_of(h * half + top, piece), piece), own_cols:] = val
+
+            @pl.when(j == 9)
+            def _():
+                lax.fori_loop(8, 10, send_wide, 0)
+
+            @pl.when((j >= 10) & (j < 14))
+            def _():
+                g_start(j, cols)
+                s_start(j)
+
+            @pl.when(j == 10)
+            def _():
+                w_wait(3)
+                w_start(11, 12)
+
+            @pl.when(j == 13)
+            def _():
+                w_wait(1)
+                w_start(9, 10)
 
             return carry
 
@@ -166,6 +272,19 @@
         pltpu.SemaphoreType.DMA,
     )
 
+    def drain_near(j, carry):
+        g_wait_send(j, own_cols)
+        return carry
+
+    def drain_wide(j, carry):
+        g_wait_send(j, cols)
+        return carry
+
+    def drain_shared(j, carry):
+        r, h = place(j)
+        s_copy(j, r, h).wait_send()
+        return carry
+
     def consume(acc, wb_sem, res_sem):
         tile_n = 512
 
@@ -175,8 +294,13 @@
 
         def add(r, h, slot, first=False, subs=(0, 1, 2, 3)):
             if r:
-                for s in subs:
-                    g_copy(0, r, h, s).wait_recv()
+                if (r, h) == (7, 1):
+                    for s in subs:
+                        last_copy(s).wait_recv()
+                else:
+                    g_copy(0, r, h, own_cols if r in (2, 3, 6, 7) else cols).wait_recv()
+            if r in (3, 6, 7) and subs[0] == 0:
+                s_copy(8, r - 2, h).wait_recv()
             count = piece * len(subs)
             inner = pl.ds(subs[0] * piece, count)
             outer = pl.ds(h * half + subs[0] * piece, count)
@@ -191,25 +315,26 @@
                 else:
                     acc[outer, tile] += prod
 
-        def res_copy(h, k):
-            return pltpu.make_async_copy(res_ref.at[pl.ds(h * half + k * chunk, chunk)], rbuf.at[k % 2], res_sem.at[k % 2])
-
-        chunk, sub = 64, 32
-
-        def finish(h, ks):
-            for k in ks:
-                res_copy(h, k).wait()
-                @pl.loop(0, chunk // sub)
-                def _(i):
-                    at = pl.multiple_of(i * sub, sub)
-                    there = pl.ds(h * half + k * chunk + at, sub)
-                    h32 = rbuf[k % 2, pl.ds(at, sub)].astype(F32) + acc[there]
-                    mean_sq = jnp.sum(h32 * h32, axis=-1, keepdims=True) * (1.0 / width)
-                    h_ref[there] = h32.astype(BF16)
-                    n_ref[there] = (h32 * lax.rsqrt(mean_sq + EPS) * gain_ref[...]).astype(BF16)
-
-                if 8 * h + k + 2 < 16:
-                    res_copy(h + (k + 2) // 8, (k + 2) % 8).start()
+        def add_residual():
+            copy = pltpu.make_async_copy(res_ref, h_ref, res_sem)
+            copy.start()
+            copy.wait()
+
+            @pl.loop(0, rows // 32)
+            def _(i):
+                at = pl.ds(pl.multiple_of(i * 32, 32), 32)
+                acc[at] += h_ref[at].astype(F32)
+
+        sub = 32
+
+        def finish(h, s0, count):
+            @pl.loop(0, count * piece // sub)
+            def _(i):
+                there = pl.ds(pl.multiple_of(h * half + s0 * piece + i * sub, sub), sub)
+                h32 = acc[there]
+                mean_sq = jnp.sum(h32 * h32, axis=-1, keepdims=True) * (1.0 / width)
+                h_ref[there] = h32.astype(BF16)
+                n_ref[there] = (h32 * lax.rsqrt(mean_sq + EPS) * gain_ref[...]).astype(BF16)
 
         def run(steps, first=False):
             load(steps[0][0], 0).start()
@@ -220,19 +345,30 @@
                 for h in halves:
                     add(r, h, i % 2, first and i == 0)
 
-        res_copy(0, 0).start()
-        res_copy(0, 1).start()
-        w_wait(5, 7)
-        w_start(13, 14, 15)
+        w_wait(5)
+        w_start(13)
         w_wait(4)
         run([(0, (0, 1)), (1, (0, 1))], first=True)
+        w_wait(7)
+        w_start(14, 15)
+        w_wait(8, 11)
+        w_start(17)
+        run([(4, (0, 1))])
+        w_wait(12, 17)
+        run([(5, (0, 1))])
         w_wait(6, 9)
         w_start(16)
-        w_wait(8, 11)
-        w_start(17)
-        run([(2, (0,)), (4, (0,))])
-        w_wait(10, 16, 12, 17)
-        run([(3, (0,)), (5, (0,)), (2, (1,)), (4, (1,)), (3, (1,)), (5, (1,))])
+        run([(2, (0, 1))])
+        w_wait(10, 16)
+        run([(3, (0, 1))])
+        for e in range(13):
+            w_copy(e).wait_send()
+        for k in range(6):
+            q_arrived(k).wait_send()
+        lax.fori_loop(0, 4, drain_near, 0)
+        lax.fori_loop(8, 12, drain_wide, 0)
+        lax.fori_loop(8, 14, drain_shared, 0)
+        add_residual()
         w_wait(13, 14)
         w_start(18)
         load(6, 0).start()
@@ -240,39 +376,34 @@
         add(6, 0, 0)
         w_wait(15, 18)
         load(7, 1).start()
+        add(6, 1, 0)
         load(7, 1).wait()
         add(7, 0, 1)
-        add(6, 1, 0)
-        finish(0, range(8))
+        finish(0, 0, 4)
         add(7, 1, 1, subs=(0, 1))
-        finish(1, range(4))
+        finish(1, 0, 2)
         add(7, 1, 1, subs=(2,))
-        finish(1, (4, 5))
+        finish(1, 2, 1)
         tail = pl.ds(rows - piece, piece)
         part_ref[...] = acc[tail]
-        res_copy(1, 6).wait()
-        res_copy(1, 7).wait()
-        g_copy(0, 7, 1, 3).wait_recv()
+        last_copy(3).wait_recv()
         act_ref[...] = gin[6, tail]
 
     pl.run_scoped(
         consume,
         pltpu.VMEM((rows, width), F32),
         pltpu.SemaphoreType.DMA((2,)),
-        pltpu.SemaphoreType.DMA((2,)),
+        pltpu.SemaphoreType.DMA,
     )
 
-    for e in range(len(events)):
+    for e in range(13, len(events)):
         w_copy(e).wait_send()
-
-    def drain(j, carry):
-        g_wait_send(j)
-        return carry
-
-    lax.fori_loop(0, 12, drain, 0)
-
-
-def tail_kernel(h_ref, n_ref, w_ref, part_ref, act_ref, res_ref, gain_ref, h_out, n_out, total, tail_h, tail_n, sem):
+    lax.fori_loop(4, 7, drain_near, 0)
+    for s in range(4):
+        last_copy(s).wait_send()
+
+
+def tail_kernel(h_ref, n_ref, w_ref, part_ref, act_ref, gain_ref, h_out, n_out, total, tail_h, tail_n, sem):
     rows, width = h_ref.shape
     piece = part_ref.shape[0]
     done, tail = pl.ds(0, rows - piece), pl.ds(rows - piece, piece)
@@ -295,8 +426,7 @@
     @pl.loop(0, piece // sub)
     def _(i):
         at = pl.ds(pl.multiple_of(i * sub, sub), sub)
-        within = pl.ds(pl.multiple_of((i % 2) * sub, sub), sub)
-        h32 = res_ref[i // 2, within].astype(F32) + total[at]
+        h32 = total[at]
         mean_sq = jnp.sum(h32 * h32, axis=-1, keepdims=True) * (1.0 / width)
         tail_h[at] = h32.astype(BF16)
         tail_n[at] = (h32 * lax.rsqrt(mean_sq + EPS) * gain_ref[...]).astype(BF16)
@@ -323,25 +453,28 @@
                 pltpu.VMEM((rows, width), BF16),
                 pltpu.VMEM((piece, width), F32),
                 pltpu.VMEM((piece, cols), BF16),
-                pltpu.VMEM((2, piece // 2, width), BF16),
                 jax.ShapeDtypeStruct((8, rows, width), BF16),
             ),
             in_specs=[any_spec] * 5 + [vm],
-            out_specs=(vm,) * 6 + (any_spec,),
+            out_specs=(vm,) * 5 + (any_spec,),
             scratch_shapes=[
                 pltpu.VMEM((14, rows // 2, cols), BF16),
                 pltpu.VMEM((7, rows, cols), BF16),
                 pltpu.SemaphoreType.DMA((19,)),
                 pltpu.SemaphoreType.DMA((19,)),
-                pltpu.SemaphoreType.DMA((64,)),
-                pltpu.SemaphoreType.DMA((64,)),
+                pltpu.SemaphoreType.DMA((18,)),
+                pltpu.SemaphoreType.DMA((20,)),
+                pltpu.SemaphoreType.DMA((12,)),
+                pltpu.SemaphoreType.DMA((12,)),
+                pltpu.SemaphoreType.DMA((6,)),
+                pltpu.SemaphoreType.DMA((12,)),
             ],
-            compiler_params=pltpu.CompilerParams(collective_id=0, has_side_effects=True, vmem_limit_bytes=45_100_000),
+            compiler_params=pltpu.CompilerParams(collective_id=0, has_side_effects=True, vmem_limit_bytes=46_200_000),
         )(x_in, w_gate, w_up, w_down, residual, gain)
         return pl.pallas_call(
             tail_kernel,
             out_shape=(jax.ShapeDtypeStruct((rows, width), BF16), jax.ShapeDtypeStruct((rows, width), BF16)),
-            in_specs=[vm] * 7,
+            in_specs=[vm] * 6,
             out_specs=(any_spec, any_spec),
             scratch_shapes=[
                 pltpu.VMEM((piece, width), F32),

time: 294 us -> 289 us (0.983)
  Pallas kernels: 293 us -> 288 us
    pallas_call x1, Pallas kernels: 289 us -> 283 us  [local_block(): pl.pallas_call(block_kernel, out_shape=(pltpu.VMEM((rows, width), BF16),...]
where the time goes in v6:
time: 289 us
  Pallas kernels  288 us (100%)
    pallas_call x1, Pallas kernels, local_block(): pl.pallas_call(block_kernel, out_shape=(pltpu.VMEM((rows, width), BF16),...  283 us

profile of v6, /device:TPU:1, one launch (start us, length us, event | category | flops | bytes accessed | tf_op | source)
XLA Modules:
  0.0 288.6 jit_solution(10394251058537976540)
XLA Ops:
  0.6 0.0 copy-start
  0.6 283.3 %shard_map.77 = (bf16[1024,3072]{1,0:T(8,128)(2,1)S(1)}, bf16[1024,3072]{1,0:T(8,128)(2,1)S(1)}, bf16[1024,3072]{1,0:T(8,128)(2,1)S(1)}, f32[128,3072]{1,0:T(8,1...) custom-call(bf16[8192,3072]{1,0:T(8,128)(2,1)} %x_ref.1, bf16[3072,1024]{1,0:T(8,128)(2,1)} %wg_ref.1, ...), custom_call_target="tpu_custom_call" | custom-call | tf_op jit(solution)/shard_map/pallas_call | solution.py:448
  284.0 0.0 copy-done
  284.0 4.6 %shard_map.78 = (bf16[1024,3072]{1,0:T(8,128)(2,1)}, bf16[1024,3072]{1,0:T(8,128)(2,1)}) custom-call(bf16[1024,3072]{1,0:T(8,128)(2,1)S(1)} %get-tuple-element.7.h_ref, bf16[1024,3072]{1,0:T(8,128)(2,1)S(1)} %get-tuple-element.8.n_ref, bf16[1024,3072]{1,0:T(8,128)(2,1)S(1)} %get-tuple-element.9.w_ref, f32[128,3072]{1,0:T(8,128)S(1)} %get-tuple-element.10.part_ref, ...), custom_call_target="tpu_custom_call" | custom-call | tf_op jit(solution)/shard_map/pallas_call | solution.py:474
Async XLA Ops:
  0.6 283.3 %copy-start = (f32[3072]{0:T(1024)S(1)}, f32[3072]{0:T(1024)}, u32[]{:S(2)}) copy-start(f32[3072]{0:T(1024)} %param.11) | copy-start | bytes 36868

commit v7 on v6

--- a/solution.py
+++ b/solution.py
@@ -65,7 +65,7 @@
     def w_copy(e):
         src, dst, where, target = events[e]
         src_ref = wd_ref.at[where] if src == 0 else wall_ref.at[src, where]
-        return pltpu.make_async_remote_copy(src_ref=src_ref, dst_ref=wall_ref.at[dst, where], send_sem=w_send.at[e], recv_sem=w_recv.at[e], device_id=target, device_id_type=MESH)
+        return pltpu.make_async_remote_copy(src_ref=src_ref, dst_ref=wall_ref.at[dst, where], send_sem=w_send.at[0], recv_sem=w_recv.at[e], device_id=target, device_id_type=MESH)
 
     def w_start(*ids):
         for e in ids:
@@ -82,7 +82,7 @@
     def g_copy(j, r, h, count):
         src = gout.at[j, :, pl.ds(0, count)]
         dst = gin.at[r - 1, pl.ds(h * half, half), pl.ds(0, count)]
-        return pltpu.make_async_remote_copy(src_ref=src, dst_ref=dst, send_sem=g_send.at[j], recv_sem=g_recv.at[2 * r + h], device_id=tp(r), device_id_type=MESH)
+        return pltpu.make_async_remote_copy(src_ref=src, dst_ref=dst, send_sem=g_send.at[jnp.where(j < 8, 0, jnp.where(j < 12, 1, j - 10))], recv_sem=g_recv.at[2 * r + h - 2], device_id=tp(r), device_id_type=MESH)
 
     def g_start(j, count):
         r, h = place(j)
@@ -96,14 +96,14 @@
         where = pl.ds(s * piece, piece)
         src = gout.at[7, where, pl.ds(0, own_cols)]
         dst = gin.at[6, pl.ds(half + s * piece, piece), pl.ds(0, own_cols)]
-        return pltpu.make_async_remote_copy(src_ref=src, dst_ref=dst, send_sem=g_send.at[14 + s], recv_sem=g_recv.at[16 + s], device_id=tp(7), device_id_type=MESH)
+        return pltpu.make_async_remote_copy(src_ref=src, dst_ref=dst, send_sem=g_send.at[0], recv_sem=g_recv.at[13 + s], device_id=tp(7), device_id_type=MESH)
 
     def stage(j):
         return jnp.where(j < 12, j - 4, j - 10)
 
     def s_copy(j, r, h):
         shared = pl.ds(own_cols, share)
-        return pltpu.make_async_remote_copy(src_ref=gout.at[stage(j), :, shared], dst_ref=gin.at[r + 1, pl.ds(h * half, half), shared], send_sem=s_send.at[j - 8], recv_sem=s_recv.at[2 * r + h], device_id=tp(r), device_id_type=MESH)
+        return pltpu.make_async_remote_copy(src_ref=gout.at[stage(j), :, shared], dst_ref=gin.at[r + 1, pl.ds(h * half, half), shared], send_sem=s_send.at[0], recv_sem=s_recv.at[2 * (r - r // 4 * 2) + h - 2], device_id=tp(r), device_id_type=MESH)
 
     def s_start(j):
         r, h = place(j)
@@ -114,7 +114,7 @@
         return wbuf.at[pl.ds(0, deep), pl.ds(pl.multiple_of(at, share), share)]
 
     def q_copy(k, src, sem, target):
-        return pltpu.make_async_remote_copy(src_ref=src, dst_ref=q_where(k), send_sem=q_send.at[sem], recv_sem=q_recv.at[sem], device_id=target, device_id_type=MESH)
+        return pltpu.make_async_remote_copy(src_ref=src, dst_ref=q_where(k), send_sem=q_send.at[1 if target is twin else 0], recv_sem=q_recv.at[sem], device_id=target, device_id_type=MESH)
 
     def q_first(k):
         src = (wg_ref, wu_ref)[k % 2]
@@ -125,7 +125,7 @@
         return q_copy(k, q_where(k), k, tp(2))
 
     def q_swap(k):
-        return q_copy(k, q_where(k), 6 + k, twin)
+        return q_copy(k, q_where(k), 6, twin)
 
     def produce(wg, wu, x_sem, wg_sem, wu_sem):
         def x_copy(j):
@@ -208,8 +208,8 @@
 
             @pl.when(j == 8)
             def _():
-                for k in range(6):
-                    q_swap(k).wait()
+                mine_q = wbuf.at[pl.ds(0, deep), pl.ds(0, depth // 2)]
+                pltpu.make_async_remote_copy(src_ref=mine_q, dst_ref=mine_q, send_sem=q_send.at[1], recv_sem=q_recv.at[6], device_id=twin, device_id_type=MESH).wait()
 
             @pl.when(j == 9)
             def _():
@@ -271,19 +271,6 @@
         pltpu.SemaphoreType.DMA,
         pltpu.SemaphoreType.DMA,
     )
-
-    def drain_near(j, carry):
-        g_wait_send(j, own_cols)
-        return carry
-
-    def drain_wide(j, carry):
-        g_wait_send(j, cols)
-        return carry
-
-    def drain_shared(j, carry):
-        r, h = place(j)
-        s_copy(j, r, h).wait_send()
-        return carry
 
     def consume(acc, wb_sem, res_sem):
         tile_n = 512
@@ -361,18 +348,15 @@
         run([(2, (0, 1))])
         w_wait(10, 16)
         run([(3, (0, 1))])
-        for e in range(13):
-            w_copy(e).wait_send()
-        for k in range(6):
-            q_arrived(k).wait_send()
-        lax.fori_loop(0, 4, drain_near, 0)
-        lax.fori_loop(8, 12, drain_wide, 0)
-        lax.fori_loop(8, 14, drain_shared, 0)
         add_residual()
+        early = pltpu.make_async_copy(wall_ref.at[6, hm], h_ref.at[hm], res_sem)
+        late = pltpu.make_async_copy(wall_ref.at[6, ho], h_ref.at[ho], wb_sem.at[0])
+        early.start()
         w_wait(13, 14)
         w_start(18)
-        load(6, 0).start()
-        load(6, 0).wait()
+        late.start()
+        early.wait()
+        late.wait()
         add(6, 0, 0)
         w_wait(15, 18)
         load(7, 1).start()
@@ -396,11 +380,14 @@
         pltpu.SemaphoreType.DMA,
     )
 
-    for e in range(13, len(events)):
-        w_copy(e).wait_send()
-    lax.fori_loop(4, 7, drain_near, 0)
-    for s in range(4):
-        last_copy(s).wait_send()
+    def sent(ref, sem):
+        pltpu.make_async_remote_copy(src_ref=ref, dst_ref=ref, send_sem=sem, recv_sem=w_recv.at[0], device_id=tp(1), device_id_type=MESH).wait_send()
+
+    sent(wall_ref.at[pl.ds(0, 7)], w_send.at[0])
+    sent(wbuf.at[pl.ds(0, deep), pl.ds(0, depth // 2)], q_send.at[0])
+    sent(gout.at[pl.ds(0, 8), :, pl.ds(0, own_cols)], g_send.at[0])
+    sent(gout.at[pl.ds(8, 4)], g_send.at[1])
+    sent(gout.at[pl.ds(0, 6), :, pl.ds(own_cols, share)], s_send.at[0])
 
 
 def tail_kernel(h_ref, n_ref, w_ref, part_ref, act_ref, gain_ref, h_out, n_out, total, tail_h, tail_n, sem):
@@ -460,14 +447,14 @@
             scratch_shapes=[
                 pltpu.VMEM((14, rows // 2, cols), BF16),
                 pltpu.VMEM((7, rows, cols), BF16),
+                pltpu.SemaphoreType.DMA((1,)),
                 pltpu.SemaphoreType.DMA((19,)),
-                pltpu.SemaphoreType.DMA((19,)),
-                pltpu.SemaphoreType.DMA((18,)),
-                pltpu.SemaphoreType.DMA((20,)),
-                pltpu.SemaphoreType.DMA((12,)),
-                pltpu.SemaphoreType.DMA((12,)),
+                pltpu.SemaphoreType.DMA((4,)),
+                pltpu.SemaphoreType.DMA((17,)),
+                pltpu.SemaphoreType.DMA((2,)),
+                pltpu.SemaphoreType.DMA((7,)),
+                pltpu.SemaphoreType.DMA((1,)),
                 pltpu.SemaphoreType.DMA((6,)),
-                pltpu.SemaphoreType.DMA((12,)),
             ],
             compiler_params=pltpu.CompilerParams(collective_id=0, has_side_effects=True, vmem_limit_bytes=46_200_000),
         )(x_in, w_gate, w_up, w_down, residual, gain)

time: 289 us -> 288 us (level)
  no operation moved by 1% of the time
where the time goes in v7:
time: 288 us
  Pallas kernels  287 us (100%)
    pallas_call x1, Pallas kernels, local_block(): pl.pallas_call(block_kernel, out_shape=(pltpu.VMEM((rows, width), BF16),...  283 us

profile of v7, /device:TPU:1, one launch (start us, length us, event | category | flops | bytes accessed | tf_op | source)
XLA Modules:
  0.0 288.0 jit_solution(13630465656332924721)
XLA Ops:
  0.6 0.0 copy-start
  0.6 282.7 %shard_map.77 = (bf16[1024,3072]{1,0:T(8,128)(2,1)S(1)}, bf16[1024,3072]{1,0:T(8,128)(2,1)S(1)}, bf16[1024,3072]{1,0:T(8,128)(2,1)S(1)}, f32[128,3072]{1,0:T(8,1...) custom-call(bf16[8192,3072]{1,0:T(8,128)(2,1)} %x_ref.1, bf16[3072,1024]{1,0:T(8,128)(2,1)} %wg_ref.1, ...), custom_call_target="tpu_custom_call" | custom-call | tf_op jit(solution)/shard_map/pallas_call | solution.py:435
  283.4 0.0 copy-done
  283.4 4.6 %shard_map.78 = (bf16[1024,3072]{1,0:T(8,128)(2,1)}, bf16[1024,3072]{1,0:T(8,128)(2,1)}) custom-call(bf16[1024,3072]{1,0:T(8,128)(2,1)S(1)} %get-tuple-element.7.h_ref, bf16[1024,3072]{1,0:T(8,128)(2,1)S(1)} %get-tuple-element.8.n_ref, bf16[1024,3072]{1,0:T(8,128)(2,1)S(1)} %get-tuple-element.9.w_ref, f32[128,3072]{1,0:T(8,128)S(1)} %get-tuple-element.10.part_ref, ...), custom_call_target="tpu_custom_call" | custom-call | tf_op jit(solution)/shard_map/pallas_call | solution.py:461
Async XLA Ops:
  0.6 282.8 %copy-start = (f32[3072]{0:T(1024)S(1)}, f32[3072]{0:T(1024)}, u32[]{:S(2)}) copy-start(f32[3072]{0:T(1024)} %param.11) | copy-start | bytes 36868

commit v8 on v7

--- a/solution.py
+++ b/solution.py
@@ -65,7 +65,12 @@
     def w_copy(e):
         src, dst, where, target = events[e]
         src_ref = wd_ref.at[where] if src == 0 else wall_ref.at[src, where]
-        return pltpu.make_async_remote_copy(src_ref=src_ref, dst_ref=wall_ref.at[dst, where], send_sem=w_send.at[0], recv_sem=w_recv.at[e], device_id=target, device_id_type=MESH)
+        return pltpu.make_async_remote_copy(src_ref=src_ref, dst_ref=wall_ref.at[dst, where], send_sem=w_send.at[0], recv_sem=w_recv.at[{9: 6, 11: 8, 14: 9, 13: 9, 16: 10, 17: 12, 18: 11, 15: 11}.get(e, e)], device_id=target, device_id_type=MESH)
+
+    def w_both(e, count):
+        pair = wall_ref.at[1, pl.ds(0, count)]
+        sem = {13: 9, 15: 11}.get(e, e)
+        pltpu.make_async_remote_copy(src_ref=pair, dst_ref=pair, send_sem=w_send.at[0], recv_sem=w_recv.at[sem], device_id=twin, device_id_type=MESH).wait_recv()
 
     def w_start(*ids):
         for e in ids:
@@ -103,7 +108,7 @@
 
     def s_copy(j, r, h):
         shared = pl.ds(own_cols, share)
-        return pltpu.make_async_remote_copy(src_ref=gout.at[stage(j), :, shared], dst_ref=gin.at[r + 1, pl.ds(h * half, half), shared], send_sem=s_send.at[0], recv_sem=s_recv.at[2 * (r - r // 4 * 2) + h - 2], device_id=tp(r), device_id_type=MESH)
+        return pltpu.make_async_remote_copy(src_ref=gout.at[stage(j), :, shared], dst_ref=gin.at[r + 1, pl.ds(h * half, half), shared], send_sem=s_send.at[0], recv_sem=s_recv.at[r - r // 4 * 2 - 1], device_id=tp(r), device_id_type=MESH)
 
     def s_start(j):
         r, h = place(j)
@@ -286,8 +291,9 @@
                         last_copy(s).wait_recv()
                 else:
                     g_copy(0, r, h, own_cols if r in (2, 3, 6, 7) else cols).wait_recv()
-            if r in (3, 6, 7) and subs[0] == 0:
-                s_copy(8, r - 2, h).wait_recv()
+            if r in (3, 6, 7) and h == 0:
+                both = gin.at[r - 1, :, pl.ds(own_cols, share)]
+                pltpu.make_async_remote_copy(src_ref=both, dst_ref=both, send_sem=s_send.at[0], recv_sem=s_recv.at[(3, 6, 7).index(r)], device_id=tp(r), device_id_type=MESH).wait_recv()
             count = piece * len(subs)
             inner = pl.ds(subs[0] * piece, count)
             outer = pl.ds(h * half + subs[0] * piece, count)
@@ -338,27 +344,27 @@
         run([(0, (0, 1)), (1, (0, 1))], first=True)
         w_wait(7)
         w_start(14, 15)
-        w_wait(8, 11)
+        w_both(8, half)
         w_start(17)
         run([(4, (0, 1))])
-        w_wait(12, 17)
+        w_both(12, rows)
         run([(5, (0, 1))])
-        w_wait(6, 9)
+        w_both(6, half)
         w_start(16)
         run([(2, (0, 1))])
-        w_wait(10, 16)
+        w_both(10, rows)
         run([(3, (0, 1))])
         add_residual()
         early = pltpu.make_async_copy(wall_ref.at[6, hm], h_ref.at[hm], res_sem)
         late = pltpu.make_async_copy(wall_ref.at[6, ho], h_ref.at[ho], wb_sem.at[0])
         early.start()
-        w_wait(13, 14)
+        w_both(13, half)
         w_start(18)
         late.start()
         early.wait()
         late.wait()
         add(6, 0, 0)
-        w_wait(15, 18)
+        w_both(15, rows)
         load(7, 1).start()
         add(6, 1, 0)
         load(7, 1).wait()
@@ -448,13 +454,13 @@
                 pltpu.VMEM((14, rows // 2, cols), BF16),
                 pltpu.VMEM((7, rows, cols), BF16),
                 pltpu.SemaphoreType.DMA((1,)),
-                pltpu.SemaphoreType.DMA((19,)),
+                pltpu.SemaphoreType.DMA((13,)),
                 pltpu.SemaphoreType.DMA((4,)),
                 pltpu.SemaphoreType.DMA((17,)),
                 pltpu.SemaphoreType.DMA((2,)),
                 pltpu.SemaphoreType.DMA((7,)),
                 pltpu.SemaphoreType.DMA((1,)),
-                pltpu.SemaphoreType.DMA((6,)),
+                pltpu.SemaphoreType.DMA((3,)),
             ],
             compiler_params=pltpu.CompilerParams(collective_id=0, has_side_effects=True, vmem_limit_bytes=46_200_000),
         )(x_in, w_gate, w_up, w_down, residual, gain)

time: 288 us -> 288 us (level)
  no operation moved by 1% of the time
where the time goes in v8:
time: 288 us
  Pallas kernels  287 us (100%)
    pallas_call x1, Pallas kernels, local_block(): pl.pallas_call(block_kernel, out_shape=(pltpu.VMEM((rows, width), BF16),...  283 us

profile of v8, /device:TPU:1, one launch (start us, length us, event | category | flops | bytes accessed | tf_op | source)
XLA Modules:
  0.0 287.9 jit_solution(7011807823390577457)
XLA Ops:
  0.6 0.0 copy-start
  0.6 282.7 %shard_map.77 = (bf16[1024,3072]{1,0:T(8,128)(2,1)S(1)}, bf16[1024,3072]{1,0:T(8,128)(2,1)S(1)}, bf16[1024,3072]{1,0:T(8,128)(2,1)S(1)}, f32[128,3072]{1,0:T(8,1...) custom-call(bf16[8192,3072]{1,0:T(8,128)(2,1)} %x_ref.1, bf16[3072,1024]{1,0:T(8,128)(2,1)} %wg_ref.1, ...), custom_call_target="tpu_custom_call" | custom-call | tf_op jit(solution)/shard_map/pallas_call | solution.py:441
  283.3 0.0 copy-done
  283.3 4.6 %shard_map.78 = (bf16[1024,3072]{1,0:T(8,128)(2,1)}, bf16[1024,3072]{1,0:T(8,128)(2,1)}) custom-call(bf16[1024,3072]{1,0:T(8,128)(2,1)S(1)} %get-tuple-element.7.h_ref, bf16[1024,3072]{1,0:T(8,128)(2,1)S(1)} %get-tuple-element.8.n_ref, bf16[1024,3072]{1,0:T(8,128)(2,1)S(1)} %get-tuple-element.9.w_ref, f32[128,3072]{1,0:T(8,128)S(1)} %get-tuple-element.10.part_ref, ...), custom_call_target="tpu_custom_call" | custom-call | tf_op jit(solution)/shard_map/pallas_call | solution.py:467
Async XLA Ops:
  0.6 282.7 %copy-start = (f32[3072]{0:T(1024)S(1)}, f32[3072]{0:T(1024)}, u32[]{:S(2)}) copy-start(f32[3072]{0:T(1024)} %param.11) | copy-start | bytes 36868
